TPU v7x, 512 devices: a whole 4x8x8 slice. The times are simulated.
512 devices in a mesh: seq: 16 (over x_hi, y), res: 32 (over z, x_lo, core).
Axes of the slice: x: 4 (x_hi: 2, x_lo: 2; x = x_hi * 2 + x_lo), y: 8, z: 8, core: 2. Of those that a mesh axis runs over, the one named last changes fastest.
Arguments:
- alignment: float32 [1024, 256, 256], P('seq', 'res'), may hold values from -100 to 100
- pair_features: float32 [256, 256, 128], P('seq', 'res'), may hold values from -100 to 100
- outer_gain: float32 [256], replicated, may hold values from 0.5 to 1.5
- w_outer_in: float32 [256, 64], replicated, may hold values from -0.375 to 0.375
- w_outer_out: float32 [1024, 128], replicated, may hold values from -0.1875 to 0.1875
- pair_gain: float32 [128], replicated, may hold values from 0.5 to 1.5
- w_bias: float32 [128, 8], replicated, may hold values from -30 to 30
- row_gain: float32 [256], replicated, may hold values from 0.5 to 1.5
- w_project: float32 [256, 1024], replicated, may hold values from -0.375 to 0.375
- w_output: float32 [256, 256], replicated, may hold values from -0.375 to 0.375
Outputs:
- alignment_out: float32 [1024, 256, 256], P('seq', 'res')
- updated_pair_array: float32 [256, 256, 128], P('seq', 'res')
All inputs are finite; a program needn't handle non-finite values.
Results may differ from a plain program's by a relative error of at most 0.00018.
Values sent between devices are 32-bit elements; how exact they have to be, the bound alone decides.
No kernel may reach another device: no remote copies, remote signals or barrier semaphores. Data moves between devices by JAX's collectives and lax.ppermute only.
A program may use at most 128 MiB of HBM per device.

v0:
```python
import functools

import jax
import jax.numpy as jnp
from jax import lax
from jax.experimental import pallas as pl
from jax.experimental.pallas import tpu as pltpu
from jax.sharding import Mesh, PartitionSpec as P


f32 = jnp.float32
bf16 = jnp.bfloat16
precise = lax.Precision.HIGHEST

SEQ = ("xh", "yh", "yl")
RES = ("zh", "zl", "xl", "core")


def dot6(a, b, dims=(((1,), (0,)), ((), ()))):
    return lax.dot_general(a, b, dims, precision=precise, preferred_element_type=f32)


def halves(x):
    high = x.astype(bf16)
    low = (x - high.astype(f32)).astype(bf16)
    return high, low


def dot_parts(a, b, dims=(((1,), (0,)), ((), ()))):
    dot = functools.partial(lax.dot_general, dimension_numbers=dims, preferred_element_type=f32)
    return dot(a[0], b[0]) + (dot(a[0], b[1]) + dot(a[1], b[0]))


def dot3(a, b, dims=(((1,), (0,)), ((), ()))):
    return dot_parts(halves(a), halves(b), dims)


def center_scale(x):
    average = jnp.mean(x, axis=-1, keepdims=True)
    centered = x - average
    variance = jnp.mean(centered * centered, axis=-1, keepdims=True)
    return centered * lax.rsqrt(variance + 1e-05)


def lane_group(shape):
    return lax.broadcasted_iota(jnp.int32, shape, len(shape) - 1) // 32


def lanes_moved(x, shift):
    rows = x.reshape(-1, 128)
    return pltpu.roll(rows, shift % 128, 1).reshape(x.shape)


def swap_groups(parts):
    group = lane_group(parts[0].shape)
    low = group % 2 == 0
    x = [None] * 4
    for a in (0, 2):
        x[a] = jnp.where(low, parts[a], lanes_moved(parts[a + 1], 32))
        x[a + 1] = jnp.where(low, lanes_moved(parts[a], -32), parts[a + 1])
    first = group < 2
    y = [None] * 4
    for a in (0, 1):
        y[a] = jnp.where(first, x[a], lanes_moved(x[a + 2], 64))
        y[a + 2] = jnp.where(first, lanes_moved(x[a], 64), x[a + 2])
    return y


def maps_kernel(rows_ref, gain_ref, weight_ref, left_ref, right_ref, maps_ref):
    normed = center_scale(rows_ref[...]) * gain_ref[...]
    maps_ref[:, :64] = dot6(normed, weight_ref[...], (((1,), (1,)), ((), ())))
    count = left_ref.shape[1]
    group = lane_group((count, 128))
    for half in range(2):
        left = jnp.zeros((count, 128), f32)
        right = jnp.zeros((count, 128), f32)
        for k in range(4):
            part = maps_ref[pl.ds(half * 4 + k, count, stride=8), :]
            left = jnp.where(group == k, lanes_moved(part, 32 * k), left)
            right = jnp.where(group == k, lanes_moved(part, 32 * k - 32), right)
        left_ref[half] = left
        right_ref[:, half * 128 : half * 128 + 128] = right


def project_kernel(own_ref, rows_ref, gain_ref, weight_ref, qkv_ref):
    normed = halves(center_scale(rows_ref[...]) * gain_ref[...])
    for t in range(3):
        block = dot_parts(normed, halves(weight_ref[:, t * 256 : t * 256 + 256]))
        if t == 0:
            block = block * 32 ** (-0.5)
        for half in range(2):
            part = block[:, half * 128 : half * 128 + 128].reshape(16, 4, 8, 128)
            moved = swap_groups([part[:, s] for s in range(4)])
            for h in range(4):
                own = moved[h].reshape(4, 4, 8, 128)
                z, x, core = half ^ own_ref[0], (h // 2) ^ own_ref[1], (h % 2) ^ own_ref[2]
                for n in range(4):
                    qkv_ref[core, x, z, t, n] = own[:, n]


def gate_kernel(rows_ref, gain_ref, weight_ref, gate_ref):
    normed = center_scale(rows_ref[...]) * gain_ref[...]
    gate_ref[...] = jax.nn.sigmoid(dot3(normed, weight_ref[...]))


def outer_kernel(
    order_ref, left_ref, own_ref, other_ref, weight_ref, out_ref, turned_ref, rows_ref, parts_ref, both_ref
):
    for r in range(4):
        both = jnp.concatenate([own_ref[r], other_ref[r]], axis=0)
        turned_ref[r] = both.T
    for y in range(32):
        for r in range(4):
            rows_ref[(y * 4 + r) * 8 : (y * 4 + r) * 8 + 8, :] = turned_ref[r, pl.ds(y, 8, stride=32), :]
    high, low = halves(rows_ref[...])
    parts_ref[:, :128] = high
    parts_ref[:, 128:] = low
    for y in range(32):
        high, low = halves(weight_ref[pl.ds(y, 32, stride=32), :])
        both_ref[y * 32 : y * 32 + 32, :128] = high
        both_ref[y * 32 : y * 32 + 32, 128:] = low
    dot = functools.partial(jnp.dot, preferred_element_type=f32)

    def step(z, carry):
        left = jnp.concatenate(
            [
                jnp.concatenate([left_ref[2 * z + k, 0], left_ref[2 * z + k, 1]], axis=0)
                for k in range(2)
            ],
            axis=1,
        )
        high, low = halves(left)
        outer = dot(parts_ref[...], jnp.concatenate([high, high], axis=0))
        outer = outer + dot(parts_ref[:, :128], low)
        blocks = []
        for k in range(2):
            own = outer[:, k * 128 : k * 128 + 128].reshape(8, 4, 32, 128)
            moved = swap_groups([own[:, y] for y in range(4)])
            blocks += [jnp.concatenate([moved[i][y] for y in range(8)], axis=1) for i in range(4)]
        high, low = halves(jnp.concatenate(blocks, axis=0))
        update = dot(high, both_ref[...])
        update = update[:, :128] + (update[:, 128:] + dot(low, both_ref[:, :128]))
        update = update.reshape(2, 4, 4, 8, 128)
        for k in range(2):
            for r in range(4):
                out_ref[2 * z + k, r] = update[k, :, r]
        return carry

    lax.fori_loop(0, 4, step, 0)


def pair_kernel(parts_ref, pair_ref, gain_ref, weight_ref, pair_out_ref, bias_ref):
    total = parts_ref[0]
    for g in range(1, 8):
        total = total + parts_ref[g]
    total = total * (1.0 / 1024.0)
    for x in range(2):
        for c in range(2):
            at = c * 8 + x * 4
            pair_out_ref[at : at + 4] = pair_ref[at : at + 4] + total[(x * 2 + c) * 4 : (x * 2 + c) * 4 + 4]
    normed = center_scale(pair_out_ref[...].reshape(128, 128)) * gain_ref[...]
    bias_ref[...] = dot6(weight_ref[...], normed, (((1,), (1,)), ((), ())))


def attend_kernel(own_ref, *refs):
    pieces, (bias_ref, out_ref, qkv_ref) = refs[:8], refs[8:]
    for k in range(8):
        z, x, core = (k // 4) ^ own_ref[0], (k // 2 % 2) ^ own_ref[1], (k % 2) ^ own_ref[2]
        qkv_ref[z * 4 + x * 2 + core] = pieces[k][...]
    bias = bias_ref[...].reshape(256, 256)
    group = lane_group((256, 128))
    dot = functools.partial(jnp.dot, preferred_element_type=f32)
    across = (((1,), (1,)), ((), ()))
    dot_across = functools.partial(
        lax.dot_general, dimension_numbers=across, preferred_element_type=f32
    )

    def residues(t, n):
        return jnp.concatenate([qkv_ref[:, t, n, z].reshape(64, 128) for z in range(4)], axis=0)

    def step(n, carry):
        query = residues(0, n)
        key_high, key_low = halves(residues(1, n))
        keys = jnp.concatenate([key_high, key_high], axis=1)
        value_high, value_low = halves(residues(2, n))
        values = jnp.concatenate([value_high, value_low], axis=1)
        mixed = jnp.zeros((256, 128), f32)
        for s in range(4):
            high, low = halves(jnp.where(group == s, query, 0.0))
            scores = dot_across(jnp.concatenate([high, low], axis=1), keys)
            scores = scores + dot_across(high, key_low) + bias
            top = jnp.max(scores, axis=-1, keepdims=True)
            weights = jnp.exp(scores - top)
            total = jnp.sum(weights, axis=-1, keepdims=True)
            high, low = halves(weights)
            both = dot(high, values)
            summed = both[:, :128] + (both[:, 128:] + dot(low, value_high))
            mixed = jnp.where(group == s, summed / total, mixed)
        out_ref[:, n] = mixed.reshape(32, 8, 128)
        return carry

    lax.fori_loop(0, 4, step, 0)


def output_kernel(mixed_ref, gate_ref, rows_ref, weight_ref, out_ref):
    columns = []
    for half in range(2):
        parts = [mixed_ref[:, half * 4 + h].reshape(16, 8, 128) for h in range(4)]
        columns.append(jnp.stack(swap_groups(parts), axis=1).reshape(512, 128))
    gated = jnp.concatenate(columns, axis=1) * gate_ref[...]
    out_ref[...] = rows_ref[...] + dot3(gated, weight_ref[...])


def shape_of(*lengths):
    return jax.ShapeDtypeStruct(lengths, f32)


def call(kernel, flops, out_shape, *args, scratch=(), scalars=0):
    specs = [pl.BlockSpec(memory_space=pltpu.SMEM)] * scalars
    specs += [pl.BlockSpec(memory_space=pltpu.VMEM)] * (len(args) - scalars)
    return pl.pallas_call(
        kernel,
        in_specs=specs,
        out_shape=out_shape,
        scratch_shapes=list(scratch),
        cost_estimate=pl.CostEstimate(flops=flops, bytes_accessed=2**20, transcendentals=0),
        compiler_params=pltpu.CompilerParams(vmem_limit_bytes=24 * 2**20),
    )(*args)


def exchanged(value, axes):
    return lax.all_to_all(value, axes, 0, 0, tiled=True)


def sent_to_all(value, axes):
    count = lax.axis_size(axes)
    return exchanged(jnp.broadcast_to(value[None], (count, *value.shape)), axes)


def on_device(
    alignment,
    pair_features,
    outer_gain,
    w_outer_in,
    w_outer_out,
    pair_gain,
    w_bias,
    row_gain,
    w_project,
    w_output,
):
    rows = alignment.reshape(512, 256)
    gain = row_gain.reshape(1, 256)
    y, z, x, core = (lax.axis_index(axis) for axis in ("yl", "zl", "xl", "core"))
    own = jnp.stack([z, x, core])
    left, right = call(
        maps_kernel,
        10**9,
        (shape_of(2, 64, 128), shape_of(64, 256)),
        rows,
        outer_gain.reshape(1, 256),
        w_outer_in.T,
        scratch=[pltpu.VMEM((512, 128), f32)],
    )
    gate = call(gate_kernel, 10**9, shape_of(512, 256), rows, gain, w_project[:, 768:])
    moved_rows = exchanged(alignment.reshape(4, 16, 8, 256), "zh").reshape(512, 256)
    left_a = lax.dynamic_index_in_dim(left, y, 0, keepdims=False)
    left_b = lax.dynamic_index_in_dim(left, 1 - y, 0, keepdims=False)
    left_a = lax.ppermute(left_a, ("yl", "xl"), [(0, 0), (1, 2), (2, 1), (3, 3)])
    left_b = lax.ppermute(left_b, ("yl", "xl"), [(0, 1), (1, 3), (2, 0), (3, 2)])
    swap = [(0, 1), (1, 0)]
    other = lax.ppermute(right, "core", swap)
    right = jnp.where(core == 0, jnp.stack([right, other]), jnp.stack([other, right]))
    left_a, left_b, moved_rows, gate = lax.optimization_barrier(
        (left_a, left_b, moved_rows, gate)
    )
    left = jnp.where(x == y, jnp.stack([left_a, left_b]), jnp.stack([left_b, left_a]))
    left_all = sent_to_all(left, ("zh", "zl")).reshape(8, 2, 64, 128)
    other = lax.ppermute(right, "xl", swap)
    right = jnp.where(x == 0, jnp.concatenate([right, other]), jnp.concatenate([other, right]))
    other = lax.ppermute(right, "yl", swap)
    qkv = call(
        project_kernel,
        4 * 10**9,
        shape_of(2, 2, 2, 3, 4, 4, 8, 128),
        own,
        moved_rows,
        gain,
        w_project[:, :768],
        scalars=1,
    )
    order, qkv = lax.optimization_barrier((own, qkv))
    far_core = lax.ppermute(qkv[1], "core", swap)
    far_x = lax.ppermute(qkv[0, 1], "xl", swap)
    parts = call(
        outer_kernel,
        4 * 10**9,
        shape_of(8, 4, 4, 8, 128),
        order,
        left_all,
        right,
        other,
        w_outer_out,
        scratch=[
            pltpu.VMEM((4, 256, 128), f32),
            pltpu.VMEM((1024, 128), f32),
            pltpu.VMEM((1024, 256), bf16),
            pltpu.VMEM((1024, 256), bf16),
        ],
        scalars=1,
    )
    parts, far_core, far_x = lax.optimization_barrier((parts, far_core, far_x))
    parts = exchanged(parts.reshape(32, 4, 8, 128), ("xh", "yh", "xl", "core"))
    pieces = [qkv[0, 0], far_core[0], far_x, lax.ppermute(far_core[1], "xl", swap)]
    moved = [lax.ppermute(p[1], "zl", swap) for p in pieces[:2]]
    kept = [p[0] for p in pieces]
    sent = [p[1] for p in pieces[2:]]
    parts, kept, sent = lax.optimization_barrier((parts, kept, sent))
    updated_pair, bias = call(
        pair_kernel,
        10**8,
        (shape_of(16, 8, 128), shape_of(8, 128)),
        parts.reshape(8, 16, 8, 128),
        pair_features,
        pair_gain.reshape(1, 128),
        w_bias.T,
    )
    bias, sent = lax.optimization_barrier((bias, sent))
    moved += [lax.ppermute(p, "zl", swap) for p in sent]
    pieces = kept + moved
    bias = exchanged(jnp.broadcast_to(bias[None], (4, 8, 128)).reshape(32, 128), RES)
    bias = bias.reshape(32, 16, 8).transpose(1, 0, 2).reshape(16, 256)
    bias = sent_to_all(bias, SEQ).reshape(16, 16, 256)
    mixed = call(
        attend_kernel,
        4 * 10**9,
        shape_of(32, 4, 8, 128),
        own,
        *pieces,
        bias,
        scratch=[pltpu.VMEM((8, 3, 4, 4, 8, 128), f32)],
        scalars=1,
    )
    mixed = exchanged(mixed, RES)
    out = call(
        output_kernel,
        10**9,
        shape_of(512, 256),
        mixed.reshape(4, 8, 4, 8, 128),
        gate,
        rows,
        w_output,
    )
    return out.reshape(alignment.shape), updated_pair


def solution(mesh):
    fine = Mesh(
        mesh.devices.reshape(2, 4, 2, 4, 2, 2, 2), ("xh", "yh", "yl", "zh", "zl", "xl", "core")
    )
    tiled = P(SEQ, RES, None)
    return jax.shard_map(
        on_device,
        mesh=fine,
        in_specs=(tiled, tiled) + (P(),) * 8,
        out_specs=(tiled, tiled),
        check_vma=False,
    )
```

profile of v0, /device:TPU:6, one launch (start us, length us, event | category | flops | bytes accessed | tf_op | source)
XLA Modules:
  0.0 164.9 jit_solution(8117665757328740414)
XLA Ops:
  0.6 10.3 %all-to-all-start = ((f32[4,16,8,256]{3,2,1,0:T(8,128)}), f32[4,16,8,256]{3,2,1,0:T(8,128)S(1)}, u32[]{:S(2)}, u32[]{:S(2)}) async-start(f32[4,16,8,256]{3,2,1,0:T(8,128)} %bitcast.53), calls=%async_computation | async-start | bytes 1048576 | tf_op jit(solution)/shard_map/all_to_all | solution.py:232
  10.9 1.1 copy-done
  12.0 0.8 copy-done.7
  12.9 0.7 copy-done.8
  13.5 0.8 shard_map.113
  14.4 0.6 dynamic-slice_bitcast_fusion
  15.0 3.7 %collective-permute-start = (f32[64,128]{1,0:T(8,128)}, f32[64,128]{1,0:T(8,128)S(1)}, u32[]{:S(2)}, u32[]{:S(2)}) collective-permute-start(f32[64,128]{1,0:T(8,128)} %get-tuple-element.57), channel_id=1, source_target_pairs={{0,0},{2,32},{32,2},{34,34},{1,1},{3,33},{33,3},{35,35},{4,4},{6,3... | collective-permute-start | bytes 98312 | tf_op jit(solution)/shard_map/ppermute | solution.py:269
  18.8 1.9 %collective-permute-start.1 = (f32[64,128]{1,0:T(8,128)S(1)}, f32[64,128]{1,0:T(8,128)S(1)}, u32[]{:S(2)}, u32[]{:S(2)}) collective-permute-start(f32[64,128]{1,0:T(8,128)S(1)} %get-tuple-element.56), channel_id=1, source_target_pairs={{0,2},{2,34},{32,0},{34,32},{1,3},{3,35},{33,1},{35,33},{4,6},{6,3... | collective-permute-start | bytes 98312 | tf_op jit(solution)/shard_map/ppermute | solution.py:270
  20.7 1.9 %collective-permute-start.2 = (f32[64,256]{1,0:T(8,128)S(1)}, f32[64,256]{1,0:T(8,128)S(1)}, u32[]{:S(2)}, u32[]{:S(2)}) collective-permute-start(f32[64,256]{1,0:T(8,128)S(1)} %get-tuple-element.30), channel_id=1, source_target_pairs={{0,1},{1,0},{2,3},{3,2},{4,5},{5,4},{6,7},{7,6},{8,9},{9,8},{10,11... | collective-permute-start | bytes 196616 | tf_op jit(solution)/shard_map/ppermute | solution.py:272
  22.8 0.6 shard_map.114.gate_ref
  23.4 0.4 collective-permute-done.2
  23.9 3.9 %collective-permute-start.3 = (f32[2,64,256]{2,1,0:T(8,128)S(1)}, f32[2,64,256]{2,1,0:T(8,128)}, u32[]{:S(2)}, u32[]{:S(2)}) collective-permute-start(f32[2,64,256]{2,1,0:T(8,128)S(1)} %maximum_select_fusion.1), channel_id=1, source_target_pairs={{0,2},{2,0},{1,3},{3,1},{4,6},{6,4},{5,7},{7,5},{8,10},{10,8},{9,1... | collective-permute-start | bytes 393224 | tf_op jit(solution)/shard_map/ppermute | solution.py:279
  27.8 0.8 broadcast_in_dim.8
  28.7 7.2 %all-to-all-start.1 = ((f32[8,2,64,128]{3,2,1,0:T(8,128)}), f32[8,2,64,128]{3,2,1,0:T(8,128)}, u32[]{:S(2)}, u32[]{:S(2)}) async-start(f32[8,2,64,128]{3,2,1,0:T(8,128)} %broadcast_in_dim.8), calls=%async_computation.1 | async-start | bytes 1048576 | tf_op jit(solution)/shard_map/all_to_all | solution.py:232
  35.9 2.1 %shard_map.115 = f32[2,2,2,3,4,4,8,128]{7,6,5,4,3,2,1,0:T(8,128)S(1)} custom-call(s32[3]{0:T(128)S(1)} %pad_add_fusion.own_ref.order_ref, f32[512,256]{1,0:T(8,128)S(1)} %bitcast.57, f32[1,256]{1,0:T(1,128)S(1)} %bitcast.65, f32[256,768]{1,0:T(8,128)S(1)} %slice.50.weight_ref), custom_call_target="tpu_custom_call" | custom-call | flops 4000000000 | bytes 1048576 | tf_op jit(solution)/shard_map/pallas_call | solution.py:221
  38.0 1.0 slice_bitcast_fusion
  39.0 1.9 %collective-permute-start.5 = (f32[2,2,3,4,4,8,128]{6,5,4,3,2,1,0:T(8,128)}, f32[2,2,3,4,4,8,128]{6,5,4,3,2,1,0:T(8,128)}, u32[]{:S(2)}, u32[]{:S(2)}) collective-permute-start(f32[2,2,3,4,4,8,128]{6,5,4,3,2,1,0:T(8,128)} %slice_bitcast_fusion), channel_id=1, source_target_pairs={{0,1},{1,0},{2,3},{3,2},{4,5},{5,4},{6,7},{7,6},{8,9},{9,8},{10,11... | collective-permute-start | bytes 2359304 | tf_op jit(solution)/shard_map/ppermute | solution.py:293
  40.9 1.0 maximum_select_fusion.own_ref
  42.0 1.9 %collective-permute-start.4 = (f32[4,64,256]{2,1,0:T(8,128)S(1)}, f32[4,64,256]{2,1,0:T(8,128)S(1)}, u32[]{:S(2)}, u32[]{:S(2)}) collective-permute-start(f32[4,64,256]{2,1,0:T(8,128)S(1)} %maximum_select_fusion.own_ref), channel_id=1, source_target_pairs={{0,32},{32,0},{1,33},{33,1},{2,34},{34,2},{3,35},{35,3},{4,36},{36... | collective-permute-start | bytes 786440 | tf_op jit(solution)/shard_map/ppermute | solution.py:281
  43.9 0.8 slice_bitcast_fusion.2
  44.7 3.5 %collective-permute-start.6 = (f32[2,3,4,4,8,128]{5,4,3,2,1,0:T(8,128)}, f32[2,3,4,4,8,128]{5,4,3,2,1,0:T(8,128)}, u32[]{:S(2)}, u32[]{:S(2)}) collective-permute-start(f32[2,3,4,4,8,128]{5,4,3,2,1,0:T(8,128)} %slice_bitcast_fusion.2), channel_id=1, source_target_pairs={{0,2},{2,0},{1,3},{3,1},{4,6},{6,4},{5,7},{7,5},{8,10},{10,8},{9,1... | collective-permute-start | bytes 1179656 | tf_op jit(solution)/shard_map/ppermute | solution.py:294
  48.2 4.4 %collective-permute-done.4.other_ref = f32[4,64,256]{2,1,0:T(8,128)S(1)} collective-permute-done((f32[4,64,256]{2,1,0:T(8,128)S(1)}, f32[4,64,256]{2,1,0:T(8,128)S(1)}, u32[]{:S(2)}, u32[]{:S(2)}) %collective-permute-start.4) | collective-permute-done | bytes 262176 | tf_op jit(solution)/shard_map/ppermute | solution.py:281
  52.6 1.0 all-to-all-done.1.left_ref
  53.6 8.4 %shard_map.116 = f32[8,4,4,8,128]{4,3,2,1,0:T(8,128)} custom-call(s32[3]{0:T(128)S(1)} %pad_add_fusion.own_ref.order_ref, f32[8,2,64,128]{3,2,1,0:T(8,128)} %all-to-all-done.1.left_ref, f32[4,64,256]{2,1,0:T(8,128)S(1)} %maximum_select_fusion.own_ref, f32[4,64,256]{2,1,0:T(8,128)S(1)} %collective-permute-done.4.other_ref, f32[1024,128]{1,0:T(8,128)S(1)} %copy-done.5), custom_call_target="tpu_custom_call" | custom-call | flops 4000000000 | bytes 1048576 | tf_op jit(solution)/shard_map/pallas_call | solution.py:221
  62.0 9.0 %all-to-all-start.2 = ((f32[32,4,8,128]{3,2,1,0:T(8,128)}), f32[32,4,8,128]{3,2,1,0:T(8,128)S(1)}, u32[]{:S(2)}, u32[]{:S(2)}) async-start(f32[32,4,8,128]{3,2,1,0:T(8,128)} %bitcast.17), calls=%async_computation.2 | async-start | bytes 1048576 | tf_op jit(solution)/shard_map/all_to_all | solution.py:232
  71.0 0.7 slice_bitcast_fusion.6
  71.8 1.1 slice_bitcast_fusion.1
  72.8 2.8 %collective-permute-start.7 = (f32[2,3,4,4,8,128]{5,4,3,2,1,0:T(8,128)S(1)}, f32[2,3,4,4,8,128]{5,4,3,2,1,0:T(8,128)S(1)}, u32[]{:S(2)}, u32[]{:S(2)}) collective-permute-start(f32[2,3,4,4,8,128]{5,4,3,2,1,0:T(8,128)S(1)} %slice_bitcast_fusion.1), channel_id=1, source_target_pairs={{0,2},{2,0},{1,3},{3,1},{4,6},{6,4},{5,7},{7,5},{8,10},{10,8},{9,1... | collective-permute-start | bytes 1179656 | tf_op jit(solution)/shard_map/ppermute | solution.py:314
  75.6 1.7 %slice_bitcast_fusion.5 = (f32[3,4,4,8,128]{4,3,2,1,0:T(8,128)}, f32[3,4,4,8,128]{4,3,2,1,0:T(8,128)S(1)}) fusion(f32[2,2,3,4,4,8,128]{6,5,4,3,2,1,0:T(8,128)} %collective-permute-done.5), kind=kLoop, calls=%fused_computation.6 | loop fusion | bytes 786432 | tf_op jit(solution)/shard_map/squeeze | solution.py:315
  77.3 1.7 %slice_bitcast_fusion.7 = (f32[3,4,4,8,128]{4,3,2,1,0:T(8,128)}, f32[3,4,4,8,128]{4,3,2,1,0:T(8,128)S(1)}) fusion(f32[2,3,4,4,8,128]{5,4,3,2,1,0:T(8,128)} %collective-permute-done.6), kind=kLoop, calls=%fused_computation.8 | loop fusion | bytes 786432 | tf_op jit(solution)/shard_map/squeeze | solution.py:317
  79.1 10.0 %collective-permute-done.7 = f32[2,3,4,4,8,128]{5,4,3,2,1,0:T(8,128)S(1)} collective-permute-done((f32[2,3,4,4,8,128]{5,4,3,2,1,0:T(8,128)S(1)}, f32[2,3,4,4,8,128]{5,4,3,2,1,0:T(8,128)S(1)}, u32[]{:S(2)}, u32[]{:S(2)}) %collective-permute-start.7) | collective-permute-done | bytes 393248 | tf_op jit(solution)/shard_map/ppermute | solution.py:314
  89.1 0.7 slice_bitcast_fusion.3
  89.8 0.8 shard_map.117
  90.6 15.3 %all_to_all.34 = f32[32,1,128]{2,1,0:T(1,128)S(1)} all-to-all(f32[32,1,128]{2,1,0:T(1,128)S(1)} %bitcast.68), channel_id=1, replica_groups=mesh['xh'=2,'yh'=4,'yl'=2,'zh'=4,'zl'=2,'xl'=2,'core'=2] {'zh','zl','xl'..., dimensions={0} | all-to-all | bytes 32768 | tf_op jit(solution)/shard_map/all_to_all | solution.py:232
  105.9 0.1 copy.19
  106.0 0.1 copy.20
  106.2 0.7 broadcast_in_dim.22
  107.0 9.3 %all-to-all-start.4 = ((f32[16,16,256]{2,1,0:T(8,128)}), f32[16,16,256]{2,1,0:T(8,128)S(1)}, u32[]{:S(2)}, u32[]{:S(2)}) async-start(f32[16,16,256]{2,1,0:T(8,128)} %broadcast_in_dim.22), calls=%async_computation.4 | async-start | bytes 524288 | tf_op jit(solution)/shard_map/all_to_all | solution.py:232
  116.3 2.5 %collective-permute-start.8 = (f32[3,4,4,8,128]{4,3,2,1,0:T(8,128)}, f32[3,4,4,8,128]{4,3,2,1,0:T(8,128)S(1)}, u32[]{:S(2)}, u32[]{:S(2)}) collective-permute-start(f32[3,4,4,8,128]{4,3,2,1,0:T(8,128)} %get-tuple-element.48), channel_id=1, source_target_pairs={{0,4},{4,0},{1,5},{5,1},{2,6},{6,2},{3,7},{7,3},{8,12},{12,8},{9,1... | collective-permute-start | bytes 589832 | tf_op jit(solution)/shard_map/ppermute | solution.py:315
  118.8 3.5 %collective-permute-start.9 = (f32[3,4,4,8,128]{4,3,2,1,0:T(8,128)}, f32[3,4,4,8,128]{4,3,2,1,0:T(8,128)S(1)}, u32[]{:S(2)}, u32[]{:S(2)}) collective-permute-start(f32[3,4,4,8,128]{4,3,2,1,0:T(8,128)} %get-tuple-element.50), channel_id=1, source_target_pairs={{0,4},{4,0},{1,5},{5,1},{2,6},{6,2},{3,7},{7,3},{8,12},{12,8},{9,1... | collective-permute-start | bytes 589832 | tf_op jit(solution)/shard_map/ppermute | solution.py:315
  122.3 2.5 %collective-permute-start.10 = (f32[3,4,4,8,128]{4,3,2,1,0:T(8,128)}, f32[3,4,4,8,128]{4,3,2,1,0:T(8,128)S(1)}, u32[]{:S(2)}, u32[]{:S(2)}) collective-permute-start(f32[3,4,4,8,128]{4,3,2,1,0:T(8,128)} %get-tuple-element.43), channel_id=1, source_target_pairs={{0,4},{4,0},{1,5},{5,1},{2,6},{6,2},{3,7},{7,3},{8,12},{12,8},{9,1... | collective-permute-start | bytes 589832 | tf_op jit(solution)/shard_map/ppermute | solution.py:329
  124.8 3.3 %collective-permute-start.11 = (f32[3,4,4,8,128]{4,3,2,1,0:T(8,128)}, f32[3,4,4,8,128]{4,3,2,1,0:T(8,128)S(1)}, u32[]{:S(2)}, u32[]{:S(2)}) collective-permute-start(f32[3,4,4,8,128]{4,3,2,1,0:T(8,128)} %get-tuple-element.44), channel_id=1, source_target_pairs={{0,4},{4,0},{1,5},{5,1},{2,6},{6,2},{3,7},{7,3},{8,12},{12,8},{9,1... | collective-permute-start | bytes 589832 | tf_op jit(solution)/shard_map/ppermute | solution.py:329
  128.1 2.2 %collective-permute-done.9.refs_5_ = f32[3,4,4,8,128]{4,3,2,1,0:T(8,128)S(1)} collective-permute-done((f32[3,4,4,8,128]{4,3,2,1,0:T(8,128)}, f32[3,4,4,8,128]{4,3,2,1,0:T(8,128)S(1)}, u32[]{:S(2)}, u32[]{:S(2)}) %collective-permute-start.9) | collective-permute-done | bytes 196640 | tf_op jit(solution)/shard_map/ppermute | solution.py:315
  130.3 4.2 %collective-permute-done.10.refs_6_ = f32[3,4,4,8,128]{4,3,2,1,0:T(8,128)S(1)} collective-permute-done((f32[3,4,4,8,128]{4,3,2,1,0:T(8,128)}, f32[3,4,4,8,128]{4,3,2,1,0:T(8,128)S(1)}, u32[]{:S(2)}, u32[]{:S(2)}) %collective-permute-start.10) | collective-permute-done | bytes 196640 | tf_op jit(solution)/shard_map/ppermute | solution.py:329
  134.5 2.4 %collective-permute-done.11.refs_7_ = f32[3,4,4,8,128]{4,3,2,1,0:T(8,128)S(1)} collective-permute-done((f32[3,4,4,8,128]{4,3,2,1,0:T(8,128)}, f32[3,4,4,8,128]{4,3,2,1,0:T(8,128)S(1)}, u32[]{:S(2)}, u32[]{:S(2)}) %collective-permute-start.11) | collective-permute-done | bytes 196640 | tf_op jit(solution)/shard_map/ppermute | solution.py:329
  137.0 4.6 %shard_map.118 = f32[32,4,8,128]{3,2,1,0:T(8,128)S(1)} custom-call(s32[3]{0:T(128)S(1)} %pad_add_fusion.own_ref.order_ref, f32[3,4,4,8,128]{4,3,2,1,0:T(8,128)S(1)} %get-tuple-element.35.refs_0_, f32[3,4,4,8,128]{4,3,2,1,0:T(8,128)S(1)} %get-tuple-element.36.refs_1_, f32[3,4,4,8,128]{4,3,2,1,0:T(8,128)S(1)} %get-tuple-element.37.refs_2_, ...), custom_call_target="tpu_custom_call" | custom-call | flops 4000000000 | bytes 1048576 | tf_op jit(solution)/shard_map/pallas_call | solution.py:221
  141.6 21.9 %all_to_all.35 = f32[32,4,8,128]{3,2,1,0:T(8,128)S(1)} all-to-all(f32[32,4,8,128]{3,2,1,0:T(8,128)S(1)} %shard_map.118), channel_id=1, replica_groups=mesh['xh'=2,'yh'=4,'yl'=2,'zh'=4,'zl'=2,'xl'=2,'core'=2] {'zh','zl','xl'..., dimensions={0} | all-to-all | bytes 1048576 | tf_op jit(solution)/shard_map/all_to_all | solution.py:232
  163.5 1.4 shard_map.119
  (39 shorter events, 0.3 us)
Async XLA Ops:
  0.6 27.2 %all-to-all-start = ((f32[4,16,8,256]{3,2,1,0:T(8,128)}), f32[4,16,8,256]{3,2,1,0:T(8,128)S(1)}, u32[]{:S(2)}, u32[]{:S(2)}) async-start(f32[4,16,8,256]{3,2,1,0:T(8,128)} %bitcast.53), calls=%async_computation | async-start | bytes 1048576 | tf_op jit(solution)/shard_map/all_to_all | solution.py:232
  10.9 1.1 copy-start
  12.0 0.8 copy-start.7
  12.9 0.7 copy-start.8
  13.5 9.1 %copy-start.12 = (f32[256,1024]{1,0:T(8,128)S(1)}, f32[256,1024]{1,0:T(8,128)}, u32[]{:S(2)}) copy-start(f32[256,1024]{1,0:T(8,128)} %param.18) | copy-start | bytes 3145732
  14.4 8.4 %copy-start.1 = (f32[64,8,256]{2,1,0:T(8,128)S(1)}, f32[64,8,256]{2,1,0:T(8,128)}, u32[]{:S(2)}) copy-start(f32[64,8,256]{2,1,0:T(8,128)} %param.10) | copy-start | bytes 1572868
  14.4 8.4 %copy-start.9 = (f32[256]{0:T(256)S(1)}, f32[256]{0:T(256)}, u32[]{:S(2)}) copy-start(f32[256]{0:T(256)} %param.17) | copy-start | bytes 3076
  15.0 12.8 %collective-permute-start = (f32[64,128]{1,0:T(8,128)}, f32[64,128]{1,0:T(8,128)S(1)}, u32[]{:S(2)}, u32[]{:S(2)}) collective-permute-start(f32[64,128]{1,0:T(8,128)} %get-tuple-element.57), channel_id=1, source_target_pairs={{0,0},{2,32},{32,2},{34,34},{1,1},{3,33},{33,3},{35,35},{4,4},{6,3... | collective-permute-start | bytes 98312 | tf_op jit(solution)/shard_map/ppermute | solution.py:269
  18.8 9.0 %collective-permute-start.1 = (f32[64,128]{1,0:T(8,128)S(1)}, f32[64,128]{1,0:T(8,128)S(1)}, u32[]{:S(2)}, u32[]{:S(2)}) collective-permute-start(f32[64,128]{1,0:T(8,128)S(1)} %get-tuple-element.56), channel_id=1, source_target_pairs={{0,2},{2,34},{32,0},{34,32},{1,3},{3,35},{33,1},{35,33},{4,6},{6,3... | collective-permute-start | bytes 98312 | tf_op jit(solution)/shard_map/ppermute | solution.py:270
  20.7 3.1 %collective-permute-start.2 = (f32[64,256]{1,0:T(8,128)S(1)}, f32[64,256]{1,0:T(8,128)S(1)}, u32[]{:S(2)}, u32[]{:S(2)}) collective-permute-start(f32[64,256]{1,0:T(8,128)S(1)} %get-tuple-element.30), channel_id=1, source_target_pairs={{0,1},{1,0},{2,3},{3,2},{4,5},{5,4},{6,7},{7,6},{8,9},{9,8},{10,11... | collective-permute-start | bytes 196616 | tf_op jit(solution)/shard_map/ppermute | solution.py:272
  23.4 5.3 %copy-start.10 = (f32[512,256]{1,0:T(8,128)}, f32[512,256]{1,0:T(8,128)S(1)}, u32[]{:S(2)}) copy-start(f32[512,256]{1,0:T(8,128)S(1)} %shard_map.114.gate_ref) | copy-start | bytes 1572868
  23.9 17.1 %collective-permute-start.3 = (f32[2,64,256]{2,1,0:T(8,128)S(1)}, f32[2,64,256]{2,1,0:T(8,128)}, u32[]{:S(2)}, u32[]{:S(2)}) collective-permute-start(f32[2,64,256]{2,1,0:T(8,128)S(1)} %maximum_select_fusion.1), channel_id=1, source_target_pairs={{0,2},{2,0},{1,3},{3,1},{4,6},{6,4},{5,7},{7,5},{8,10},{10,8},{9,1... | collective-permute-start | bytes 393224 | tf_op jit(solution)/shard_map/ppermute | solution.py:279
  28.7 24.9 %all-to-all-start.1 = ((f32[8,2,64,128]{3,2,1,0:T(8,128)}), f32[8,2,64,128]{3,2,1,0:T(8,128)}, u32[]{:S(2)}, u32[]{:S(2)}) async-start(f32[8,2,64,128]{3,2,1,0:T(8,128)} %broadcast_in_dim.8), calls=%async_computation.1 | async-start | bytes 1048576 | tf_op jit(solution)/shard_map/all_to_all | solution.py:232
  38.0 15.6 %copy-start.5 = (f32[1024,128]{1,0:T(8,128)S(1)}, f32[1024,128]{1,0:T(8,128)}, u32[]{:S(2)}) copy-start(f32[1024,128]{1,0:T(8,128)} %weight_ref.2) | copy-start | bytes 1572868
  39.0 23.0 %collective-permute-start.5 = (f32[2,2,3,4,4,8,128]{6,5,4,3,2,1,0:T(8,128)}, f32[2,2,3,4,4,8,128]{6,5,4,3,2,1,0:T(8,128)}, u32[]{:S(2)}, u32[]{:S(2)}) collective-permute-start(f32[2,2,3,4,4,8,128]{6,5,4,3,2,1,0:T(8,128)} %slice_bitcast_fusion), channel_id=1, source_target_pairs={{0,1},{1,0},{2,3},{3,2},{4,5},{5,4},{6,7},{7,6},{8,9},{9,8},{10,11... | collective-permute-start | bytes 2359304 | tf_op jit(solution)/shard_map/ppermute | solution.py:293
  42.0 10.6 %collective-permute-start.4 = (f32[4,64,256]{2,1,0:T(8,128)S(1)}, f32[4,64,256]{2,1,0:T(8,128)S(1)}, u32[]{:S(2)}, u32[]{:S(2)}) collective-permute-start(f32[4,64,256]{2,1,0:T(8,128)S(1)} %maximum_select_fusion.own_ref), channel_id=1, source_target_pairs={{0,32},{32,0},{1,33},{33,1},{2,34},{34,2},{3,35},{35,3},{4,36},{36... | collective-permute-start | bytes 786440 | tf_op jit(solution)/shard_map/ppermute | solution.py:281
  44.7 17.3 %collective-permute-start.6 = (f32[2,3,4,4,8,128]{5,4,3,2,1,0:T(8,128)}, f32[2,3,4,4,8,128]{5,4,3,2,1,0:T(8,128)}, u32[]{:S(2)}, u32[]{:S(2)}) collective-permute-start(f32[2,3,4,4,8,128]{5,4,3,2,1,0:T(8,128)} %slice_bitcast_fusion.2), channel_id=1, source_target_pairs={{0,2},{2,0},{1,3},{3,1},{4,6},{6,4},{5,7},{7,5},{8,10},{10,8},{9,1... | collective-permute-start | bytes 1179656 | tf_op jit(solution)/shard_map/ppermute | solution.py:294
  62.0 27.8 %all-to-all-start.2 = ((f32[32,4,8,128]{3,2,1,0:T(8,128)}), f32[32,4,8,128]{3,2,1,0:T(8,128)S(1)}, u32[]{:S(2)}, u32[]{:S(2)}) async-start(f32[32,4,8,128]{3,2,1,0:T(8,128)} %bitcast.17), calls=%async_computation.2 | async-start | bytes 1048576 | tf_op jit(solution)/shard_map/all_to_all | solution.py:232
  71.8 18.0 %copy-start.2 = (f32[16,8,128]{2,1,0:T(8,128)S(1)}, f32[16,8,128]{2,1,0:T(8,128)}, u32[]{:S(2)}) copy-start(f32[16,8,128]{2,1,0:T(8,128)} %pair_ref.1) | copy-start | bytes 196612
  71.8 18.0 %copy-start.3 = (f32[128,8]{0,1:T(8,128)S(1)}, f32[128,8]{0,1:T(8,128)}, u32[]{:S(2)}) copy-start(f32[128,8]{0,1:T(8,128)} %param.16) | copy-start | bytes 12292
  71.8 18.0 %copy-start.4 = (f32[128]{0:T(128)S(1)}, f32[128]{0:T(128)}, u32[]{:S(2)}) copy-start(f32[128]{0:T(128)} %param.15) | copy-start | bytes 1540
  72.8 16.2 %collective-permute-start.7 = (f32[2,3,4,4,8,128]{5,4,3,2,1,0:T(8,128)S(1)}, f32[2,3,4,4,8,128]{5,4,3,2,1,0:T(8,128)S(1)}, u32[]{:S(2)}, u32[]{:S(2)}) collective-permute-start(f32[2,3,4,4,8,128]{5,4,3,2,1,0:T(8,128)S(1)} %slice_bitcast_fusion.1), channel_id=1, source_target_pairs={{0,2},{2,0},{1,3},{3,1},{4,6},{6,4},{5,7},{7,5},{8,10},{10,8},{9,1... | collective-permute-start | bytes 1179656 | tf_op jit(solution)/shard_map/ppermute | solution.py:314
  107.0 30.0 %all-to-all-start.4 = ((f32[16,16,256]{2,1,0:T(8,128)}), f32[16,16,256]{2,1,0:T(8,128)S(1)}, u32[]{:S(2)}, u32[]{:S(2)}) async-start(f32[16,16,256]{2,1,0:T(8,128)} %broadcast_in_dim.22), calls=%async_computation.4 | async-start | bytes 524288 | tf_op jit(solution)/shard_map/all_to_all | solution.py:232
  116.3 11.9 %collective-permute-start.8 = (f32[3,4,4,8,128]{4,3,2,1,0:T(8,128)}, f32[3,4,4,8,128]{4,3,2,1,0:T(8,128)S(1)}, u32[]{:S(2)}, u32[]{:S(2)}) collective-permute-start(f32[3,4,4,8,128]{4,3,2,1,0:T(8,128)} %get-tuple-element.48), channel_id=1, source_target_pairs={{0,4},{4,0},{1,5},{5,1},{2,6},{6,2},{3,7},{7,3},{8,12},{12,8},{9,1... | collective-permute-start | bytes 589832 | tf_op jit(solution)/shard_map/ppermute | solution.py:315
  118.8 44.7 %copy-start.6 = (f32[256,256]{1,0:T(8,128)S(1)}, f32[256,256]{1,0:T(8,128)}, u32[]{:S(2)}) copy-start(f32[256,256]{1,0:T(8,128)} %weight_ref.3) | copy-start | bytes 786436
  118.8 44.7 %copy-start.11 = (f32[512,256]{1,0:T(8,128)S(1)}, f32[512,256]{1,0:T(8,128)}, u32[]{:S(2)}) copy-start(f32[512,256]{1,0:T(8,128)} %copy-done.10) | copy-start | bytes 1572868
  118.8 11.5 %collective-permute-start.9 = (f32[3,4,4,8,128]{4,3,2,1,0:T(8,128)}, f32[3,4,4,8,128]{4,3,2,1,0:T(8,128)S(1)}, u32[]{:S(2)}, u32[]{:S(2)}) collective-permute-start(f32[3,4,4,8,128]{4,3,2,1,0:T(8,128)} %get-tuple-element.50), channel_id=1, source_target_pairs={{0,4},{4,0},{1,5},{5,1},{2,6},{6,2},{3,7},{7,3},{8,12},{12,8},{9,1... | collective-permute-start | bytes 589832 | tf_op jit(solution)/shard_map/ppermute | solution.py:315
  122.3 12.3 %collective-permute-start.10 = (f32[3,4,4,8,128]{4,3,2,1,0:T(8,128)}, f32[3,4,4,8,128]{4,3,2,1,0:T(8,128)S(1)}, u32[]{:S(2)}, u32[]{:S(2)}) collective-permute-start(f32[3,4,4,8,128]{4,3,2,1,0:T(8,128)} %get-tuple-element.43), channel_id=1, source_target_pairs={{0,4},{4,0},{1,5},{5,1},{2,6},{6,2},{3,7},{7,3},{8,12},{12,8},{9,1... | collective-permute-start | bytes 589832 | tf_op jit(solution)/shard_map/ppermute | solution.py:329
  124.8 12.2 %collective-permute-start.11 = (f32[3,4,4,8,128]{4,3,2,1,0:T(8,128)}, f32[3,4,4,8,128]{4,3,2,1,0:T(8,128)S(1)}, u32[]{:S(2)}, u32[]{:S(2)}) collective-permute-start(f32[3,4,4,8,128]{4,3,2,1,0:T(8,128)} %get-tuple-element.44), channel_id=1, source_target_pairs={{0,4},{4,0},{1,5},{5,1},{2,6},{6,2},{3,7},{7,3},{8,12},{12,8},{9,1... | collective-permute-start | bytes 589832 | tf_op jit(solution)/shard_map/ppermute | solution.py:329
where the time goes:
time: 166 us; the launch traced here: 165 us
  starting transfers between devices  69.3 us (42%)
  blocking collectives  37.2 us (22%)
  waiting for transfers between devices  24.6 us (15%)
  Pallas kernels  18.7 us (11%)
  local copies, waits for them, and re-layouts  12.9 us (8%)
    all_to_all x2, blocking collectives, exchanged(): return lax.all_to_all(value, axes, 0, 0, tiled=True)  37.2 us
    all_to_all x4, starting transfers between devices, exchanged(): return lax.all_to_all(value, axes, 0, 0, tiled=True)  35.9 us
    pallas_call x7, Pallas kernels, call(): pl.pallas_call(kernel, in_specs=specs, out_shape=out_shape, scratch_shape...  18.7 us
    ppermute x1, waiting for transfers between devices, on_device(): lax.ppermute(far_core[1], 'xl', swap)  10 us
    ppermute x2, waiting for transfers between devices, on_device(): moved += [lax.ppermute(p, 'zl', swap) for p in sent]  6.64 us
    ppermute x2, starting transfers between devices, on_device(): moved = [lax.ppermute(p[1], 'zl', swap) for p in pieces[:2]]  5.96 us
    ppermute x2, starting transfers between devices, on_device(): moved += [lax.ppermute(p, 'zl', swap) for p in sent]  5.84 us
    ppermute x1, waiting for transfers between devices, on_device(): other = lax.ppermute(right, 'yl', swap)  4.37 us
  transfers between devices with their start and end apart: 16, of which 7 were waited for; matrix products, arithmetic and copies ran while one was open for 6% of the time, Pallas kernels for 7%

commit v1 on v0

--- a/solution.py
+++ b/solution.py
@@ -121,7 +121,7 @@
         both_ref[y * 32 : y * 32 + 32, 128:] = low
     dot = functools.partial(jnp.dot, preferred_element_type=f32)
 
-    def step(z, carry):
+    for z in range(4):
         left = jnp.concatenate(
             [
                 jnp.concatenate([left_ref[2 * z + k, 0], left_ref[2 * z + k, 1]], axis=0)
@@ -144,9 +144,6 @@
         for k in range(2):
             for r in range(4):
                 out_ref[2 * z + k, r] = update[k, :, r]
-        return carry
-
-    lax.fori_loop(0, 4, step, 0)
 
 
 def pair_kernel(parts_ref, pair_ref, gain_ref, weight_ref, pair_out_ref, bias_ref):
@@ -159,7 +156,9 @@
             at = c * 8 + x * 4
             pair_out_ref[at : at + 4] = pair_ref[at : at + 4] + total[(x * 2 + c) * 4 : (x * 2 + c) * 4 + 4]
     normed = center_scale(pair_out_ref[...].reshape(128, 128)) * gain_ref[...]
-    bias_ref[...] = dot6(weight_ref[...], normed, (((1,), (1,)), ((), ())))
+    bias = dot6(weight_ref[...], normed, (((1,), (1,)), ((), ())))
+    for copy in range(4):
+        bias_ref[copy] = bias
 
 
 def attend_kernel(own_ref, *refs):
@@ -262,7 +261,6 @@
         w_outer_in.T,
         scratch=[pltpu.VMEM((512, 128), f32)],
     )
-    gate = call(gate_kernel, 10**9, shape_of(512, 256), rows, gain, w_project[:, 768:])
     moved_rows = exchanged(alignment.reshape(4, 16, 8, 256), "zh").reshape(512, 256)
     left_a = lax.dynamic_index_in_dim(left, y, 0, keepdims=False)
     left_b = lax.dynamic_index_in_dim(left, 1 - y, 0, keepdims=False)
@@ -271,9 +269,7 @@
     swap = [(0, 1), (1, 0)]
     other = lax.ppermute(right, "core", swap)
     right = jnp.where(core == 0, jnp.stack([right, other]), jnp.stack([other, right]))
-    left_a, left_b, moved_rows, gate = lax.optimization_barrier(
-        (left_a, left_b, moved_rows, gate)
-    )
+    left_a, left_b, moved_rows = lax.optimization_barrier((left_a, left_b, moved_rows))
     left = jnp.where(x == y, jnp.stack([left_a, left_b]), jnp.stack([left_b, left_a]))
     left_all = sent_to_all(left, ("zh", "zl")).reshape(8, 2, 64, 128)
     other = lax.ppermute(right, "xl", swap)
@@ -312,24 +308,26 @@
     parts, far_core, far_x = lax.optimization_barrier((parts, far_core, far_x))
     parts = exchanged(parts.reshape(32, 4, 8, 128), ("xh", "yh", "xl", "core"))
     pieces = [qkv[0, 0], far_core[0], far_x, lax.ppermute(far_core[1], "xl", swap)]
-    moved = [lax.ppermute(p[1], "zl", swap) for p in pieces[:2]]
+    moved = [lax.ppermute(p[1], "zl", swap) for p in pieces[:3]]
     kept = [p[0] for p in pieces]
-    sent = [p[1] for p in pieces[2:]]
+    sent = pieces[3][1]
     parts, kept, sent = lax.optimization_barrier((parts, kept, sent))
     updated_pair, bias = call(
         pair_kernel,
         10**8,
-        (shape_of(16, 8, 128), shape_of(8, 128)),
+        (shape_of(16, 8, 128), shape_of(4, 8, 128)),
         parts.reshape(8, 16, 8, 128),
         pair_features,
         pair_gain.reshape(1, 128),
         w_bias.T,
     )
-    bias, sent = lax.optimization_barrier((bias, sent))
-    moved += [lax.ppermute(p, "zl", swap) for p in sent]
+    bias, sent, late_gain = lax.optimization_barrier((bias, sent, gain))
+    gate = call(gate_kernel, 10**9, shape_of(512, 256), rows, late_gain, w_project[:, 768:])
+    moved.append(lax.ppermute(sent, "zl", swap))
     pieces = kept + moved
-    bias = exchanged(jnp.broadcast_to(bias[None], (4, 8, 128)).reshape(32, 128), RES)
+    bias = exchanged(bias.reshape(32, 128), RES)
     bias = bias.reshape(32, 16, 8).transpose(1, 0, 2).reshape(16, 256)
+    bias, pieces, gate = lax.optimization_barrier((bias, pieces, gate))
     bias = sent_to_all(bias, SEQ).reshape(16, 16, 256)
     mixed = call(
         attend_kernel,

time: 166 us -> 159 us (0.958)
  the two profiles are of different devices: /device:TPU:6 before, /device:TPU:8 now
where the time goes in v1:
time: 159 us; the launch traced here: 157 us
  starting transfers between devices  69.2 us (44%)
  blocking collectives  43 us (27%)
  Pallas kernels  15.8 us (10%)
  waiting for transfers between devices  15.6 us (10%)
  local copies, waits for them, and re-layouts  11.8 us (7%)
    all_to_all x2, blocking collectives, exchanged(): return lax.all_to_all(value, axes, 0, 0, tiled=True)  43 us
    all_to_all x4, starting transfers between devices, exchanged(): return lax.all_to_all(value, axes, 0, 0, tiled=True)  34.8 us
    pallas_call x7, Pallas kernels, call(): pl.pallas_call(kernel, in_specs=specs, out_shape=out_shape, scratch_shape...  15.8 us
    ppermute x3, starting transfers between devices, on_device(): moved = [lax.ppermute(p[1], 'zl', swap) for p in pieces[:3]]  9.47 us
    all_to_all x4, waiting for transfers between devices, exchanged(): return lax.all_to_all(value, axes, 0, 0, tiled=True)  8.46 us
    squeeze x3, local copies, waits for them, and re-layouts, on_device(): moved = [lax.ppermute(p[1], 'zl', swap) for p in pieces[:3]]  4.17 us
    ppermute x1, starting transfers between devices, on_device(): far_x = lax.ppermute(qkv[0, 1], 'xl', swap)  3.92 us
    ppermute x1, starting transfers between devices, on_device(): other = lax.ppermute(right, 'xl', swap)  3.92 us
  transfers between devices with their start and end apart: 16, of which 5 were waited for; matrix products, arithmetic and copies ran while one was open for 6% of the time, Pallas kernels for 6%

profile of v1, /device:TPU:8, one launch (start us, length us, event | category | flops | bytes accessed | tf_op | source)
XLA Modules:
  0.0 157.5 jit_solution(2381222052204873973)
XLA Ops:
  0.6 10.3 %all-to-all-start = ((f32[4,16,8,256]{3,2,1,0:T(8,128)}), f32[4,16,8,256]{3,2,1,0:T(8,128)S(1)}, u32[]{:S(2)}, u32[]{:S(2)}) async-start(f32[4,16,8,256]{3,2,1,0:T(8,128)} %bitcast.53), calls=%async_computation | async-start | bytes 1048576 | tf_op jit(solution)/shard_map/all_to_all | solution.py:231
  10.9 1.1 copy-done
  12.0 0.8 copy-done.7
  12.9 0.7 copy-done.8
  13.5 0.8 shard_map.113
  14.4 3.3 %collective-permute-start = (f32[64,128]{1,0:T(8,128)S(1)}, f32[64,128]{1,0:T(8,128)S(1)}, u32[]{:S(2)}, u32[]{:S(2)}) collective-permute-start(f32[64,128]{1,0:T(8,128)S(1)} %get-tuple-element.73), channel_id=1, source_target_pairs={{0,0},{2,32},{32,2},{34,34},{1,1},{3,33},{33,3},{35,35},{4,4},{6,3... | collective-permute-start | bytes 98312 | tf_op jit(solution)/shard_map/ppermute | solution.py:267
  17.7 1.9 %collective-permute-start.1 = (f32[64,128]{1,0:T(8,128)S(1)}, f32[64,128]{1,0:T(8,128)S(1)}, u32[]{:S(2)}, u32[]{:S(2)}) collective-permute-start(f32[64,128]{1,0:T(8,128)S(1)} %get-tuple-element.72), channel_id=1, source_target_pairs={{0,2},{2,34},{32,0},{34,32},{1,3},{3,35},{33,1},{35,33},{4,6},{6,3... | collective-permute-start | bytes 98312 | tf_op jit(solution)/shard_map/ppermute | solution.py:268
  19.6 1.9 %collective-permute-start.2 = (f32[64,256]{1,0:T(8,128)S(1)}, f32[64,256]{1,0:T(8,128)S(1)}, u32[]{:S(2)}, u32[]{:S(2)}) collective-permute-start(f32[64,256]{1,0:T(8,128)S(1)} %get-tuple-element.38), channel_id=1, source_target_pairs={{0,1},{1,0},{2,3},{3,2},{4,5},{5,4},{6,7},{7,6},{8,9},{9,8},{10,11... | collective-permute-start | bytes 196616 | tf_op jit(solution)/shard_map/ppermute | solution.py:270
  21.6 0.1 slice.49.weight_ref
  21.7 0.1 pad_add_fusion.own_ref.order_ref
  21.7 1.0 collective-permute-done.2
  22.8 3.9 %collective-permute-start.3 = (f32[2,64,256]{2,1,0:T(8,128)S(1)}, f32[2,64,256]{2,1,0:T(8,128)}, u32[]{:S(2)}, u32[]{:S(2)}) collective-permute-start(f32[2,64,256]{2,1,0:T(8,128)S(1)} %maximum_select_fusion.1), channel_id=1, source_target_pairs={{0,2},{2,0},{1,3},{3,1},{4,6},{6,4},{5,7},{7,5},{8,10},{10,8},{9,1... | collective-permute-start | bytes 393224 | tf_op jit(solution)/shard_map/ppermute | solution.py:275
  26.8 0.8 broadcast_in_dim.4
  27.6 7.2 %all-to-all-start.1 = ((f32[8,2,64,128]{3,2,1,0:T(8,128)}), f32[8,2,64,128]{3,2,1,0:T(8,128)S(1)}, u32[]{:S(2)}, u32[]{:S(2)}) async-start(f32[8,2,64,128]{3,2,1,0:T(8,128)} %broadcast_in_dim.4), calls=%async_computation.1 | async-start | bytes 1048576 | tf_op jit(solution)/shard_map/all_to_all | solution.py:231
  34.8 2.1 %shard_map.114 = f32[2,2,2,3,4,4,8,128]{7,6,5,4,3,2,1,0:T(8,128)S(1)} custom-call(s32[3]{0:T(128)S(1)} %pad_add_fusion.own_ref.order_ref, f32[512,256]{1,0:T(8,128)S(1)} %bitcast.57, f32[1,256]{1,0:T(1,128)S(1)} %bitcast.64, f32[256,768]{1,0:T(8,128)S(1)} %slice.49.weight_ref), custom_call_target="tpu_custom_call" | custom-call | flops 4000000000 | bytes 1048576 | tf_op jit(solution)/shard_map/pallas_call | solution.py:220
  36.9 0.0 copy-start.5
  36.9 1.0 slice_bitcast_fusion
  37.9 1.9 %collective-permute-start.5 = (f32[2,2,3,4,4,8,128]{6,5,4,3,2,1,0:T(8,128)}, f32[2,2,3,4,4,8,128]{6,5,4,3,2,1,0:T(8,128)}, u32[]{:S(2)}, u32[]{:S(2)}) collective-permute-start(f32[2,2,3,4,4,8,128]{6,5,4,3,2,1,0:T(8,128)} %slice_bitcast_fusion), channel_id=1, source_target_pairs={{0,1},{1,0},{2,3},{3,2},{4,5},{5,4},{6,7},{7,6},{8,9},{9,8},{10,11... | collective-permute-start | bytes 2359304 | tf_op jit(solution)/shard_map/ppermute | solution.py:289
  39.9 1.0 maximum_select_fusion.own_ref
  40.9 2.0 %collective-permute-start.4 = (f32[4,64,256]{2,1,0:T(8,128)S(1)}, f32[4,64,256]{2,1,0:T(8,128)S(1)}, u32[]{:S(2)}, u32[]{:S(2)}) collective-permute-start(f32[4,64,256]{2,1,0:T(8,128)S(1)} %maximum_select_fusion.own_ref), channel_id=1, source_target_pairs={{0,32},{32,0},{1,33},{33,1},{2,34},{34,2},{3,35},{35,3},{4,36},{36... | collective-permute-start | bytes 786440 | tf_op jit(solution)/shard_map/ppermute | solution.py:277
  42.9 0.8 slice_bitcast_fusion.2
  43.7 3.9 %collective-permute-start.6 = (f32[2,3,4,4,8,128]{5,4,3,2,1,0:T(8,128)}, f32[2,3,4,4,8,128]{5,4,3,2,1,0:T(8,128)}, u32[]{:S(2)}, u32[]{:S(2)}) collective-permute-start(f32[2,3,4,4,8,128]{5,4,3,2,1,0:T(8,128)} %slice_bitcast_fusion.2), channel_id=1, source_target_pairs={{0,2},{2,0},{1,3},{3,1},{4,6},{6,4},{5,7},{7,5},{8,10},{10,8},{9,1... | collective-permute-start | bytes 1179656 | tf_op jit(solution)/shard_map/ppermute | solution.py:290
  47.6 3.9 %collective-permute-done.4.other_ref = f32[4,64,256]{2,1,0:T(8,128)S(1)} collective-permute-done((f32[4,64,256]{2,1,0:T(8,128)S(1)}, f32[4,64,256]{2,1,0:T(8,128)S(1)}, u32[]{:S(2)}, u32[]{:S(2)}) %collective-permute-start.4) | collective-permute-done | bytes 262176 | tf_op jit(solution)/shard_map/ppermute | solution.py:277
  51.5 0.9 all-to-all-done.1.left_ref
  52.4 5.3 %shard_map.115 = f32[8,4,4,8,128]{4,3,2,1,0:T(8,128)} custom-call(s32[3]{0:T(128)S(1)} %pad_add_fusion.own_ref.order_ref, f32[8,2,64,128]{3,2,1,0:T(8,128)S(1)} %all-to-all-done.1.left_ref, f32[4,64,256]{2,1,0:T(8,128)S(1)} %maximum_select_fusion.own_ref, f32[4,64,256]{2,1,0:T(8,128)S(1)} %collective-permute-done.4.other_ref, f32[1024,128]{1,0:T(8,128)S(1)} %copy-done.5), custom_call_target="tpu_custom_call" | custom-call | flops 4000000000 | bytes 1048576 | tf_op jit(solution)/shard_map/pallas_call | solution.py:220
  57.7 9.7 %all-to-all-start.2 = ((f32[32,4,8,128]{3,2,1,0:T(8,128)}), f32[32,4,8,128]{3,2,1,0:T(8,128)S(1)}, u32[]{:S(2)}, u32[]{:S(2)}) async-start(f32[32,4,8,128]{3,2,1,0:T(8,128)} %bitcast.17), calls=%async_computation.2 | async-start | bytes 1048576 | tf_op jit(solution)/shard_map/all_to_all | solution.py:231
  67.4 0.7 slice_bitcast_fusion.7
  68.1 3.7 %collective-permute-start.8 = (f32[3,4,4,8,128]{4,3,2,1,0:T(8,128)}, f32[3,4,4,8,128]{4,3,2,1,0:T(8,128)S(1)}, u32[]{:S(2)}, u32[]{:S(2)}) collective-permute-start(f32[3,4,4,8,128]{4,3,2,1,0:T(8,128)} %get-tuple-element.64), channel_id=1, source_target_pairs={{0,4},{4,0},{1,5},{5,1},{2,6},{6,2},{3,7},{7,3},{8,12},{12,8},{9,1... | collective-permute-start | bytes 589832 | tf_op jit(solution)/shard_map/ppermute | solution.py:311
  71.7 1.0 slice_bitcast_fusion.1
  72.8 3.8 %collective-permute-start.7 = (f32[2,3,4,4,8,128]{5,4,3,2,1,0:T(8,128)S(1)}, f32[2,3,4,4,8,128]{5,4,3,2,1,0:T(8,128)S(1)}, u32[]{:S(2)}, u32[]{:S(2)}) collective-permute-start(f32[2,3,4,4,8,128]{5,4,3,2,1,0:T(8,128)S(1)} %slice_bitcast_fusion.1), channel_id=1, source_target_pairs={{0,2},{2,0},{1,3},{3,1},{4,6},{6,4},{5,7},{7,5},{8,10},{10,8},{9,1... | collective-permute-start | bytes 1179656 | tf_op jit(solution)/shard_map/ppermute | solution.py:310
  76.6 1.7 %slice_bitcast_fusion.6 = (f32[3,4,4,8,128]{4,3,2,1,0:T(8,128)}, f32[3,4,4,8,128]{4,3,2,1,0:T(8,128)S(1)}) fusion(f32[2,2,3,4,4,8,128]{6,5,4,3,2,1,0:T(8,128)} %collective-permute-done.5), kind=kLoop, calls=%fused_computation.7 | loop fusion | bytes 786432 | tf_op jit(solution)/shard_map/squeeze | solution.py:311
  78.4 2.3 %collective-permute-start.9 = (f32[3,4,4,8,128]{4,3,2,1,0:T(8,128)}, f32[3,4,4,8,128]{4,3,2,1,0:T(8,128)S(1)}, u32[]{:S(2)}, u32[]{:S(2)}) collective-permute-start(f32[3,4,4,8,128]{4,3,2,1,0:T(8,128)} %get-tuple-element.66), channel_id=1, source_target_pairs={{0,4},{4,0},{1,5},{5,1},{2,6},{6,2},{3,7},{7,3},{8,12},{12,8},{9,1... | collective-permute-start | bytes 589832 | tf_op jit(solution)/shard_map/ppermute | solution.py:311
  80.7 1.7 %slice_bitcast_fusion.5 = (f32[3,4,4,8,128]{4,3,2,1,0:T(8,128)}, f32[3,4,4,8,128]{4,3,2,1,0:T(8,128)S(1)}) fusion(f32[2,3,4,4,8,128]{5,4,3,2,1,0:T(8,128)} %collective-permute-done.6), kind=kLoop, calls=%fused_computation.6 | loop fusion | bytes 786432 | tf_op jit(solution)/shard_map/squeeze | solution.py:311
  82.4 3.5 %collective-permute-start.10 = (f32[3,4,4,8,128]{4,3,2,1,0:T(8,128)}, f32[3,4,4,8,128]{4,3,2,1,0:T(8,128)S(1)}, u32[]{:S(2)}, u32[]{:S(2)}) collective-permute-start(f32[3,4,4,8,128]{4,3,2,1,0:T(8,128)} %get-tuple-element.68), channel_id=1, source_target_pairs={{0,4},{4,0},{1,5},{5,1},{2,6},{6,2},{3,7},{7,3},{8,12},{12,8},{9,1... | collective-permute-start | bytes 589832 | tf_op jit(solution)/shard_map/ppermute | solution.py:311
  85.9 2.2 %collective-permute-done.7 = f32[2,3,4,4,8,128]{5,4,3,2,1,0:T(8,128)S(1)} collective-permute-done((f32[2,3,4,4,8,128]{5,4,3,2,1,0:T(8,128)S(1)}, f32[2,3,4,4,8,128]{5,4,3,2,1,0:T(8,128)S(1)}, u32[]{:S(2)}, u32[]{:S(2)}) %collective-permute-start.7) | collective-permute-done | bytes 393248 | tf_op jit(solution)/shard_map/ppermute | solution.py:310
  88.2 1.0 shard_map.116
  89.2 2.2 %collective-permute-start.11 = (f32[3,4,4,8,128]{4,3,2,1,0:T(8,128)S(1)}, f32[3,4,4,8,128]{4,3,2,1,0:T(8,128)S(1)}, u32[]{:S(2)}, u32[]{:S(2)}) collective-permute-start(f32[3,4,4,8,128]{4,3,2,1,0:T(8,128)S(1)} %get-tuple-element.51), channel_id=1, source_target_pairs={{0,4},{4,0},{1,5},{5,1},{2,6},{6,2},{3,7},{7,3},{8,12},{12,8},{9,1... | collective-permute-start | bytes 589832 | tf_op jit(solution)/shard_map/ppermute | solution.py:326
  91.4 1.0 slice.61.weight_ref
  92.3 7.6 %all-to-all-start.3 = ((f32[32,1,128]{2,1,0:T(1,128)}), f32[32,1,128]{2,1,0:T(1,128)S(1)}, u32[]{:S(2)}, u32[]{:S(2)}) async-start(f32[32,1,128]{2,1,0:T(1,128)} %bitcast.28), calls=%async_computation.3 | async-start | bytes 32768 | tf_op jit(solution)/shard_map/all_to_all | solution.py:231
  100.0 0.6 shard_map.117.gate_ref
  100.6 7.6 %all-to-all-done.3 = f32[32,1,128]{2,1,0:T(1,128)S(1)} async-done(((f32[32,1,128]{2,1,0:T(1,128)}), f32[32,1,128]{2,1,0:T(1,128)S(1)}, u32[]{:S(2)}, u32[]{:S(2)}) %all-to-all-start.3) | async-done | bytes 16416 | tf_op jit(solution)/shard_map/all_to_all | solution.py:231
  108.1 0.1 copy.17
  108.2 0.1 copy.18
  108.4 0.1 copy.19
  108.5 22.0 %all_to_all.34.refs_8_ = f32[16,16,256]{2,1,0:T(8,128)S(1)} all-to-all(f32[16,16,256]{2,1,0:T(8,128)S(1)} %broadcast_in_dim.5), channel_id=1, replica_groups=mesh['xh'=2,'yh'=4,'yl'=2,'zh'=4,'zl'=2,'xl'=2,'core'=2] {'xh','yh','yl'}, dimensions={0} | all-to-all | bytes 524288 | tf_op jit(solution)/shard_map/all_to_all | solution.py:231
  130.5 4.6 %shard_map.118 = f32[32,4,8,128]{3,2,1,0:T(8,128)S(1)} custom-call(s32[3]{0:T(128)S(1)} %pad_add_fusion.own_ref.order_ref, f32[3,4,4,8,128]{4,3,2,1,0:T(8,128)S(1)} %get-tuple-element.53.refs_0_, f32[3,4,4,8,128]{4,3,2,1,0:T(8,128)S(1)} %get-tuple-element.54.refs_1_, f32[3,4,4,8,128]{4,3,2,1,0:T(8,128)S(1)} %get-tuple-element.55.refs_2_, ...), custom_call_target="tpu_custom_call" | custom-call | flops 4000000000 | bytes 1048576 | tf_op jit(solution)/shard_map/pallas_call | solution.py:220
  135.1 21.0 %all_to_all.35 = f32[32,4,8,128]{3,2,1,0:T(8,128)S(1)} all-to-all(f32[32,4,8,128]{3,2,1,0:T(8,128)S(1)} %shard_map.118), channel_id=1, replica_groups=mesh['xh'=2,'yh'=4,'yl'=2,'zh'=4,'zl'=2,'xl'=2,'core'=2] {'zh','zl','xl'..., dimensions={0} | all-to-all | bytes 1048576 | tf_op jit(solution)/shard_map/all_to_all | solution.py:231
  156.1 1.4 shard_map.119
  (34 shorter events, 0.2 us)
Async XLA Ops:
  0.6 26.1 %all-to-all-start = ((f32[4,16,8,256]{3,2,1,0:T(8,128)}), f32[4,16,8,256]{3,2,1,0:T(8,128)S(1)}, u32[]{:S(2)}, u32[]{:S(2)}) async-start(f32[4,16,8,256]{3,2,1,0:T(8,128)} %bitcast.53), calls=%async_computation | async-start | bytes 1048576 | tf_op jit(solution)/shard_map/all_to_all | solution.py:231
  10.9 1.1 copy-start
  12.0 0.8 copy-start.7
  12.9 0.7 copy-start.8
  13.5 8.0 %copy-start.10 = (f32[256,1024]{1,0:T(8,128)S(1)}, f32[256,1024]{1,0:T(8,128)}, u32[]{:S(2)}) copy-start(f32[256,1024]{1,0:T(8,128)} %param.18) | copy-start | bytes 3145732
  14.4 12.3 %collective-permute-start = (f32[64,128]{1,0:T(8,128)S(1)}, f32[64,128]{1,0:T(8,128)S(1)}, u32[]{:S(2)}, u32[]{:S(2)}) collective-permute-start(f32[64,128]{1,0:T(8,128)S(1)} %get-tuple-element.73), channel_id=1, source_target_pairs={{0,0},{2,32},{32,2},{34,34},{1,1},{3,33},{33,3},{35,35},{4,4},{6,3... | collective-permute-start | bytes 98312 | tf_op jit(solution)/shard_map/ppermute | solution.py:267
  17.7 9.0 %collective-permute-start.1 = (f32[64,128]{1,0:T(8,128)S(1)}, f32[64,128]{1,0:T(8,128)S(1)}, u32[]{:S(2)}, u32[]{:S(2)}) collective-permute-start(f32[64,128]{1,0:T(8,128)S(1)} %get-tuple-element.72), channel_id=1, source_target_pairs={{0,2},{2,34},{32,0},{34,32},{1,3},{3,35},{33,1},{35,33},{4,6},{6,3... | collective-permute-start | bytes 98312 | tf_op jit(solution)/shard_map/ppermute | solution.py:268
  19.6 3.1 %collective-permute-start.2 = (f32[64,256]{1,0:T(8,128)S(1)}, f32[64,256]{1,0:T(8,128)S(1)}, u32[]{:S(2)}, u32[]{:S(2)}) collective-permute-start(f32[64,256]{1,0:T(8,128)S(1)} %get-tuple-element.38), channel_id=1, source_target_pairs={{0,1},{1,0},{2,3},{3,2},{4,5},{5,4},{6,7},{7,6},{8,9},{9,8},{10,11... | collective-permute-start | bytes 196616 | tf_op jit(solution)/shard_map/ppermute | solution.py:270
  21.6 13.3 %copy-start.9 = (f32[256]{0:T(256)S(1)}, f32[256]{0:T(256)}, u32[]{:S(2)}) copy-start(f32[256]{0:T(256)} %param.17) | copy-start | bytes 3076
  22.8 17.1 %collective-permute-start.3 = (f32[2,64,256]{2,1,0:T(8,128)S(1)}, f32[2,64,256]{2,1,0:T(8,128)}, u32[]{:S(2)}, u32[]{:S(2)}) collective-permute-start(f32[2,64,256]{2,1,0:T(8,128)S(1)} %maximum_select_fusion.1), channel_id=1, source_target_pairs={{0,2},{2,0},{1,3},{3,1},{4,6},{6,4},{5,7},{7,5},{8,10},{10,8},{9,1... | collective-permute-start | bytes 393224 | tf_op jit(solution)/shard_map/ppermute | solution.py:275
  27.6 24.8 %all-to-all-start.1 = ((f32[8,2,64,128]{3,2,1,0:T(8,128)}), f32[8,2,64,128]{3,2,1,0:T(8,128)S(1)}, u32[]{:S(2)}, u32[]{:S(2)}) async-start(f32[8,2,64,128]{3,2,1,0:T(8,128)} %broadcast_in_dim.4), calls=%async_computation.1 | async-start | bytes 1048576 | tf_op jit(solution)/shard_map/all_to_all | solution.py:231
  36.9 15.4 %copy-start.5 = (f32[1024,128]{1,0:T(8,128)S(1)}, f32[1024,128]{1,0:T(8,128)}, u32[]{:S(2)}) copy-start(f32[1024,128]{1,0:T(8,128)} %weight_ref.2) | copy-start | bytes 1572868
  37.9 19.8 %collective-permute-start.5 = (f32[2,2,3,4,4,8,128]{6,5,4,3,2,1,0:T(8,128)}, f32[2,2,3,4,4,8,128]{6,5,4,3,2,1,0:T(8,128)}, u32[]{:S(2)}, u32[]{:S(2)}) collective-permute-start(f32[2,2,3,4,4,8,128]{6,5,4,3,2,1,0:T(8,128)} %slice_bitcast_fusion), channel_id=1, source_target_pairs={{0,1},{1,0},{2,3},{3,2},{4,5},{5,4},{6,7},{7,6},{8,9},{9,8},{10,11... | collective-permute-start | bytes 2359304 | tf_op jit(solution)/shard_map/ppermute | solution.py:289
  40.9 10.6 %collective-permute-start.4 = (f32[4,64,256]{2,1,0:T(8,128)S(1)}, f32[4,64,256]{2,1,0:T(8,128)S(1)}, u32[]{:S(2)}, u32[]{:S(2)}) collective-permute-start(f32[4,64,256]{2,1,0:T(8,128)S(1)} %maximum_select_fusion.own_ref), channel_id=1, source_target_pairs={{0,32},{32,0},{1,33},{33,1},{2,34},{34,2},{3,35},{35,3},{4,36},{36... | collective-permute-start | bytes 786440 | tf_op jit(solution)/shard_map/ppermute | solution.py:277
  43.7 14.0 %collective-permute-start.6 = (f32[2,3,4,4,8,128]{5,4,3,2,1,0:T(8,128)}, f32[2,3,4,4,8,128]{5,4,3,2,1,0:T(8,128)}, u32[]{:S(2)}, u32[]{:S(2)}) collective-permute-start(f32[2,3,4,4,8,128]{5,4,3,2,1,0:T(8,128)} %slice_bitcast_fusion.2), channel_id=1, source_target_pairs={{0,2},{2,0},{1,3},{3,1},{4,6},{6,4},{5,7},{7,5},{8,10},{10,8},{9,1... | collective-permute-start | bytes 1179656 | tf_op jit(solution)/shard_map/ppermute | solution.py:290
  57.7 30.4 %all-to-all-start.2 = ((f32[32,4,8,128]{3,2,1,0:T(8,128)}), f32[32,4,8,128]{3,2,1,0:T(8,128)S(1)}, u32[]{:S(2)}, u32[]{:S(2)}) async-start(f32[32,4,8,128]{3,2,1,0:T(8,128)} %bitcast.17), calls=%async_computation.2 | async-start | bytes 1048576 | tf_op jit(solution)/shard_map/all_to_all | solution.py:231
  68.1 20.1 %copy-start.2 = (f32[16,8,128]{2,1,0:T(8,128)S(1)}, f32[16,8,128]{2,1,0:T(8,128)}, u32[]{:S(2)}) copy-start(f32[16,8,128]{2,1,0:T(8,128)} %pair_ref.1) | copy-start | bytes 196612
  68.1 20.1 %copy-start.3 = (f32[128,8]{0,1:T(8,128)S(1)}, f32[128,8]{0,1:T(8,128)}, u32[]{:S(2)}) copy-start(f32[128,8]{0,1:T(8,128)} %param.16) | copy-start | bytes 12292
  68.1 20.1 %copy-start.4 = (f32[128]{0:T(128)S(1)}, f32[128]{0:T(128)}, u32[]{:S(2)}) copy-start(f32[128]{0:T(128)} %param.15) | copy-start | bytes 1540
  68.1 40.3 %collective-permute-start.8 = (f32[3,4,4,8,128]{4,3,2,1,0:T(8,128)}, f32[3,4,4,8,128]{4,3,2,1,0:T(8,128)S(1)}, u32[]{:S(2)}, u32[]{:S(2)}) collective-permute-start(f32[3,4,4,8,128]{4,3,2,1,0:T(8,128)} %get-tuple-element.64), channel_id=1, source_target_pairs={{0,4},{4,0},{1,5},{5,1},{2,6},{6,2},{3,7},{7,3},{8,12},{12,8},{9,1... | collective-permute-start | bytes 589832 | tf_op jit(solution)/shard_map/ppermute | solution.py:311
  72.8 27.2 %copy-start.1 = (f32[64,8,256]{2,1,0:T(8,128)S(1)}, f32[64,8,256]{2,1,0:T(8,128)}, u32[]{:S(2)}) copy-start(f32[64,8,256]{2,1,0:T(8,128)} %param.10) | copy-start | bytes 1572868
  72.8 15.3 %collective-permute-start.7 = (f32[2,3,4,4,8,128]{5,4,3,2,1,0:T(8,128)S(1)}, f32[2,3,4,4,8,128]{5,4,3,2,1,0:T(8,128)S(1)}, u32[]{:S(2)}, u32[]{:S(2)}) collective-permute-start(f32[2,3,4,4,8,128]{5,4,3,2,1,0:T(8,128)S(1)} %slice_bitcast_fusion.1), channel_id=1, source_target_pairs={{0,2},{2,0},{1,3},{3,1},{4,6},{6,4},{5,7},{7,5},{8,10},{10,8},{9,1... | collective-permute-start | bytes 1179656 | tf_op jit(solution)/shard_map/ppermute | solution.py:310
  78.4 30.0 %collective-permute-start.9 = (f32[3,4,4,8,128]{4,3,2,1,0:T(8,128)}, f32[3,4,4,8,128]{4,3,2,1,0:T(8,128)S(1)}, u32[]{:S(2)}, u32[]{:S(2)}) collective-permute-start(f32[3,4,4,8,128]{4,3,2,1,0:T(8,128)} %get-tuple-element.66), channel_id=1, source_target_pairs={{0,4},{4,0},{1,5},{5,1},{2,6},{6,2},{3,7},{7,3},{8,12},{12,8},{9,1... | collective-permute-start | bytes 589832 | tf_op jit(solution)/shard_map/ppermute | solution.py:311
  82.4 26.0 %collective-permute-start.10 = (f32[3,4,4,8,128]{4,3,2,1,0:T(8,128)}, f32[3,4,4,8,128]{4,3,2,1,0:T(8,128)S(1)}, u32[]{:S(2)}, u32[]{:S(2)}) collective-permute-start(f32[3,4,4,8,128]{4,3,2,1,0:T(8,128)} %get-tuple-element.68), channel_id=1, source_target_pairs={{0,4},{4,0},{1,5},{5,1},{2,6},{6,2},{3,7},{7,3},{8,12},{12,8},{9,1... | collective-permute-start | bytes 589832 | tf_op jit(solution)/shard_map/ppermute | solution.py:311
  89.2 19.2 %collective-permute-start.11 = (f32[3,4,4,8,128]{4,3,2,1,0:T(8,128)S(1)}, f32[3,4,4,8,128]{4,3,2,1,0:T(8,128)S(1)}, u32[]{:S(2)}, u32[]{:S(2)}) collective-permute-start(f32[3,4,4,8,128]{4,3,2,1,0:T(8,128)S(1)} %get-tuple-element.51), channel_id=1, source_target_pairs={{0,4},{4,0},{1,5},{5,1},{2,6},{6,2},{3,7},{7,3},{8,12},{12,8},{9,1... | collective-permute-start | bytes 589832 | tf_op jit(solution)/shard_map/ppermute | solution.py:326
  92.3 15.8 %all-to-all-start.3 = ((f32[32,1,128]{2,1,0:T(1,128)}), f32[32,1,128]{2,1,0:T(1,128)S(1)}, u32[]{:S(2)}, u32[]{:S(2)}) async-start(f32[32,1,128]{2,1,0:T(1,128)} %bitcast.28), calls=%async_computation.3 | async-start | bytes 32768 | tf_op jit(solution)/shard_map/all_to_all | solution.py:231
  130.5 25.6 %copy-start.6 = (f32[256,256]{1,0:T(8,128)S(1)}, f32[256,256]{1,0:T(8,128)}, u32[]{:S(2)}) copy-start(f32[256,256]{1,0:T(8,128)} %weight_ref.3) | copy-start | bytes 786436

commit v2 on v1

--- a/solution.py
+++ b/solution.py
@@ -162,7 +162,8 @@
 
 
 def attend_kernel(own_ref, *refs):
-    pieces, (bias_ref, out_ref, qkv_ref) = refs[:8], refs[8:]
+    kept, moved, (bias_ref, out_ref, qkv_ref) = refs[:4], refs[4:6], refs[6:]
+    pieces = list(kept) + [moved[k % 2].at[k // 2] for k in range(4)]
     for k in range(8):
         z, x, core = (k // 4) ^ own_ref[0], (k // 2 % 2) ^ own_ref[1], (k % 2) ^ own_ref[2]
         qkv_ref[z * 4 + x * 2 + core] = pieces[k][...]
@@ -305,12 +306,12 @@
         ],
         scalars=1,
     )
-    parts, far_core, far_x = lax.optimization_barrier((parts, far_core, far_x))
+    parts, far_core = lax.optimization_barrier((parts, far_core))
     parts = exchanged(parts.reshape(32, 4, 8, 128), ("xh", "yh", "xl", "core"))
-    pieces = [qkv[0, 0], far_core[0], far_x, lax.ppermute(far_core[1], "xl", swap)]
-    moved = [lax.ppermute(p[1], "zl", swap) for p in pieces[:3]]
-    kept = [p[0] for p in pieces]
-    sent = pieces[3][1]
+    last = lax.ppermute(far_core[1], "xl", swap)
+    moved = lax.ppermute(jnp.stack([qkv[0, 0, 1], far_x[1]]), "zl", swap)
+    kept = [qkv[0, 0, 0], far_core[0, 0], far_x[0], last[0]]
+    sent = jnp.stack([far_core[0, 1], last[1]])
     parts, kept, sent = lax.optimization_barrier((parts, kept, sent))
     updated_pair, bias = call(
         pair_kernel,
@@ -321,14 +322,14 @@
         pair_gain.reshape(1, 128),
         w_bias.T,
     )
-    bias, sent, late_gain = lax.optimization_barrier((bias, sent, gain))
-    gate = call(gate_kernel, 10**9, shape_of(512, 256), rows, late_gain, w_project[:, 768:])
-    moved.append(lax.ppermute(sent, "zl", swap))
-    pieces = kept + moved
+    bias, sent = lax.optimization_barrier((bias, sent))
+    pieces = kept + [moved, lax.ppermute(sent, "zl", swap)]
     bias = exchanged(bias.reshape(32, 128), RES)
     bias = bias.reshape(32, 16, 8).transpose(1, 0, 2).reshape(16, 256)
-    bias, pieces, gate = lax.optimization_barrier((bias, pieces, gate))
+    late_gain, bias = lax.optimization_barrier((gain, bias))
+    gate = call(gate_kernel, 10**9, shape_of(512, 256), rows, late_gain, w_project[:, 768:])
     bias = sent_to_all(bias, SEQ).reshape(16, 16, 256)
+    bias, gate = lax.optimization_barrier((bias, gate))
     mixed = call(
         attend_kernel,
         4 * 10**9,

time: 159 us -> 160 us (level)
  the two profiles are of different devices: /device:TPU:8 before, /device:TPU:6 now
where the time goes in v2:
time: 160 us; the launch traced here: 159 us
  starting transfers between devices  63.2 us (40%)
  waiting for transfers between devices  37.2 us (23%)
  blocking collectives  32.8 us (20%)
  Pallas kernels  15.7 us (10%)
  local copies, waits for them, and re-layouts  7.43 us (5%)
  other arithmetic  1.66 us (1%)
    all_to_all x4, starting transfers between devices, exchanged(): return lax.all_to_all(value, axes, 0, 0, tiled=True)  36.5 us
    all_to_all x2, blocking collectives, exchanged(): return lax.all_to_all(value, axes, 0, 0, tiled=True)  32.8 us
    pallas_call x7, Pallas kernels, call(): pl.pallas_call(kernel, in_specs=specs, out_shape=out_shape, scratch_shape...  15.7 us
    ppermute x1, waiting for transfers between devices, on_device(): last = lax.ppermute(far_core[1], 'xl', swap)  14 us
    all_to_all x4, waiting for transfers between devices, exchanged(): return lax.all_to_all(value, axes, 0, 0, tiled=True)  9.27 us
    ppermute x1, waiting for transfers between devices, on_device(): pieces = kept + [moved, lax.ppermute(sent, 'zl', swap)]  6.62 us
    ppermute x1, waiting for transfers between devices, on_device(): moved = lax.ppermute(jnp.stack([qkv[0, 0, 1], far_x[1]]), 'zl', swap)  5.58 us
    ppermute x1, starting transfers between devices, on_device(): lax.ppermute(left_a, ('yl', 'xl'), [(0, 0), (1, 2), (2, 1), (3, 3)])  4.12 us
  transfers between devices with their start and end apart: 14, of which 7 were waited for; matrix products, arithmetic and copies ran while one was open for 3% of the time, Pallas kernels for 6%

profile of v2, /device:TPU:6, one launch (start us, length us, event | category | flops | bytes accessed | tf_op | source)
XLA Modules:
  0.0 159.0 jit_solution(2717499544828161386)
XLA Ops:
  0.6 10.3 %all-to-all-start = ((f32[4,16,8,256]{3,2,1,0:T(8,128)}), f32[4,16,8,256]{3,2,1,0:T(8,128)S(1)}, u32[]{:S(2)}, u32[]{:S(2)}) async-start(f32[4,16,8,256]{3,2,1,0:T(8,128)} %bitcast.49), calls=%async_computation | async-start | bytes 1048576 | tf_op jit(solution)/shard_map/all_to_all | solution.py:232
  10.9 1.1 copy-done
  12.0 0.8 copy-done.7
  12.9 0.7 copy-done.8
  13.5 0.8 shard_map.113
  14.4 1.9 %collective-permute-start.2 = (f32[64,256]{1,0:T(8,128)S(1)}, f32[64,256]{1,0:T(8,128)S(1)}, u32[]{:S(2)}, u32[]{:S(2)}) collective-permute-start(f32[64,256]{1,0:T(8,128)S(1)} %get-tuple-element.30), channel_id=1, source_target_pairs={{0,1},{1,0},{2,3},{3,2},{4,5},{5,4},{6,7},{7,6},{8,9},{9,8},{10,11... | collective-permute-start | bytes 196616 | tf_op jit(solution)/shard_map/ppermute | solution.py:271
  16.3 1.2 collective-permute-done.2
  17.5 2.7 %collective-permute-start.3 = (f32[2,64,256]{2,1,0:T(8,128)S(1)}, f32[2,64,256]{2,1,0:T(8,128)S(1)}, u32[]{:S(2)}, u32[]{:S(2)}) collective-permute-start(f32[2,64,256]{2,1,0:T(8,128)S(1)} %maximum_select_fusion.1), channel_id=1, source_target_pairs={{0,2},{2,0},{1,3},{3,1},{4,6},{6,4},{5,7},{7,5},{8,10},{10,8},{9,1... | collective-permute-start | bytes 393224 | tf_op jit(solution)/shard_map/ppermute | solution.py:276
  20.3 4.1 %collective-permute-start = (f32[64,128]{1,0:T(8,128)S(1)}, f32[64,128]{1,0:T(8,128)S(1)}, u32[]{:S(2)}, u32[]{:S(2)}) collective-permute-start(f32[64,128]{1,0:T(8,128)S(1)} %get-tuple-element.57), channel_id=1, source_target_pairs={{0,0},{2,32},{32,2},{34,34},{1,1},{3,33},{33,3},{35,35},{4,4},{6,3... | collective-permute-start | bytes 98312 | tf_op jit(solution)/shard_map/ppermute | solution.py:268
  24.4 1.9 %collective-permute-start.1 = (f32[64,128]{1,0:T(8,128)S(1)}, f32[64,128]{1,0:T(8,128)S(1)}, u32[]{:S(2)}, u32[]{:S(2)}) collective-permute-start(f32[64,128]{1,0:T(8,128)S(1)} %get-tuple-element.56), channel_id=1, source_target_pairs={{0,2},{2,34},{32,0},{34,32},{1,3},{3,35},{33,1},{35,33},{4,6},{6,3... | collective-permute-start | bytes 98312 | tf_op jit(solution)/shard_map/ppermute | solution.py:269
  26.4 0.0 copy-start.9
  26.4 0.1 slice.39.weight_ref
  26.5 0.1 pad_add_fusion.own_ref.order_ref
  26.6 3.2 %collective-permute-start.4 = (f32[4,64,256]{2,1,0:T(8,128)S(1)}, f32[4,64,256]{2,1,0:T(8,128)S(1)}, u32[]{:S(2)}, u32[]{:S(2)}) collective-permute-start(f32[4,64,256]{2,1,0:T(8,128)S(1)} %maximum_select_fusion.own_ref), channel_id=1, source_target_pairs={{0,32},{32,0},{1,33},{33,1},{2,34},{34,2},{3,35},{35,3},{4,36},{36... | collective-permute-start | bytes 786440 | tf_op jit(solution)/shard_map/ppermute | solution.py:278
  29.8 0.5 collective-permute-done.1
  30.3 0.8 broadcast_in_dim.4
  31.1 7.2 %all-to-all-start.1 = ((f32[8,2,64,128]{3,2,1,0:T(8,128)}), f32[8,2,64,128]{3,2,1,0:T(8,128)S(1)}, u32[]{:S(2)}, u32[]{:S(2)}) async-start(f32[8,2,64,128]{3,2,1,0:T(8,128)} %broadcast_in_dim.4), calls=%async_computation.1 | async-start | bytes 1048576 | tf_op jit(solution)/shard_map/all_to_all | solution.py:232
  38.3 2.1 %shard_map.114 = f32[2,2,2,3,4,4,8,128]{7,6,5,4,3,2,1,0:T(8,128)S(1)} custom-call(s32[3]{0:T(128)S(1)} %pad_add_fusion.own_ref.order_ref, f32[512,256]{1,0:T(8,128)S(1)} %bitcast.53, f32[1,256]{1,0:T(1,128)S(1)} %bitcast.61, f32[256,768]{1,0:T(8,128)S(1)} %slice.39.weight_ref), custom_call_target="tpu_custom_call" | custom-call | flops 4000000000 | bytes 1048576 | tf_op jit(solution)/shard_map/pallas_call | solution.py:221
  40.4 0.9 slice_bitcast_fusion
  41.4 1.9 %collective-permute-start.5 = (f32[2,2,3,4,4,8,128]{6,5,4,3,2,1,0:T(8,128)}, f32[2,2,3,4,4,8,128]{6,5,4,3,2,1,0:T(8,128)S(1)}, u32[]{:S(2)}, u32[]{:S(2)}) collective-permute-start(f32[2,2,3,4,4,8,128]{6,5,4,3,2,1,0:T(8,128)} %slice_bitcast_fusion), channel_id=1, source_target_pairs={{0,1},{1,0},{2,3},{3,2},{4,5},{5,4},{6,7},{7,6},{8,9},{9,8},{10,11... | collective-permute-start | bytes 2359304 | tf_op jit(solution)/shard_map/ppermute | solution.py:290
  43.3 0.8 slice_bitcast_fusion.2
  44.1 2.2 %collective-permute-start.6 = (f32[2,3,4,4,8,128]{5,4,3,2,1,0:T(8,128)}, f32[2,3,4,4,8,128]{5,4,3,2,1,0:T(8,128)S(1)}, u32[]{:S(2)}, u32[]{:S(2)}) collective-permute-start(f32[2,3,4,4,8,128]{5,4,3,2,1,0:T(8,128)} %slice_bitcast_fusion.2), channel_id=1, source_target_pairs={{0,2},{2,0},{1,3},{3,1},{4,6},{6,4},{5,7},{7,5},{8,10},{10,8},{9,1... | collective-permute-start | bytes 1179656 | tf_op jit(solution)/shard_map/ppermute | solution.py:291
  46.4 8.2 %all-to-all-done.1.left_ref = f32[8,2,64,128]{3,2,1,0:T(8,128)S(1)} async-done(((f32[8,2,64,128]{3,2,1,0:T(8,128)}), f32[8,2,64,128]{3,2,1,0:T(8,128)S(1)}, u32[]{:S(2)}, u32[]{:S(2)}) %all-to-all-start.1) | async-done | bytes 524320 | tf_op jit(solution)/shard_map/all_to_all | solution.py:232
  54.6 5.4 %shard_map.115 = f32[8,4,4,8,128]{4,3,2,1,0:T(8,128)} custom-call(s32[3]{0:T(128)S(1)} %pad_add_fusion.own_ref.order_ref, f32[8,2,64,128]{3,2,1,0:T(8,128)S(1)} %all-to-all-done.1.left_ref, f32[4,64,256]{2,1,0:T(8,128)S(1)} %maximum_select_fusion.own_ref, f32[4,64,256]{2,1,0:T(8,128)S(1)} %collective-permute-done.4.other_ref, f32[1024,128]{1,0:T(8,128)S(1)} %copy-done.5), custom_call_target="tpu_custom_call" | custom-call | flops 4000000000 | bytes 1048576 | tf_op jit(solution)/shard_map/pallas_call | solution.py:221
  60.0 9.9 %all-to-all-start.2 = ((f32[32,4,8,128]{3,2,1,0:T(8,128)}), f32[32,4,8,128]{3,2,1,0:T(8,128)S(1)}, u32[]{:S(2)}, u32[]{:S(2)}) async-start(f32[32,4,8,128]{3,2,1,0:T(8,128)} %bitcast.16), calls=%async_computation.2 | async-start | bytes 1048576 | tf_op jit(solution)/shard_map/all_to_all | solution.py:232
  70.0 0.0 copy-start.3
  70.0 0.0 copy-start.4
  70.0 2.9 %collective-permute-start.7 = (f32[2,3,4,4,8,128]{5,4,3,2,1,0:T(8,128)S(1)}, f32[2,3,4,4,8,128]{5,4,3,2,1,0:T(8,128)S(1)}, u32[]{:S(2)}, u32[]{:S(2)}) collective-permute-start(f32[2,3,4,4,8,128]{5,4,3,2,1,0:T(8,128)S(1)} %slice_bitcast_fusion.1), channel_id=1, source_target_pairs={{0,2},{2,0},{1,3},{3,1},{4,6},{6,4},{5,7},{7,5},{8,10},{10,8},{9,1... | collective-permute-start | bytes 1179656 | tf_op jit(solution)/shard_map/ppermute | solution.py:311
  73.0 14.0 %collective-permute-done.7 = f32[2,3,4,4,8,128]{5,4,3,2,1,0:T(8,128)S(1)} collective-permute-done((f32[2,3,4,4,8,128]{5,4,3,2,1,0:T(8,128)S(1)}, f32[2,3,4,4,8,128]{5,4,3,2,1,0:T(8,128)S(1)}, u32[]{:S(2)}, u32[]{:S(2)}) %collective-permute-start.7) | collective-permute-done | bytes 393248 | tf_op jit(solution)/shard_map/ppermute | solution.py:311
  87.0 0.8 pad_maximum_fusion
  87.8 0.8 shard_map.116
  88.6 10.9 %all_to_all.34 = f32[32,1,128]{2,1,0:T(1,128)S(1)} all-to-all(f32[32,1,128]{2,1,0:T(1,128)S(1)} %bitcast.56), channel_id=1, replica_groups=mesh['xh'=2,'yh'=4,'yl'=2,'zh'=4,'zl'=2,'xl'=2,'core'=2] {'zh','zl','xl'..., dimensions={0} | all-to-all | bytes 32768 | tf_op jit(solution)/shard_map/all_to_all | solution.py:232
  99.5 0.1 copy.17
  99.6 0.1 copy.18
  99.7 0.1 copy.19
  99.8 0.7 broadcast_in_dim.5
  100.5 9.0 %all-to-all-start.4 = ((f32[16,16,256]{2,1,0:T(8,128)}), f32[16,16,256]{2,1,0:T(8,128)S(1)}, u32[]{:S(2)}, u32[]{:S(2)}) async-start(f32[16,16,256]{2,1,0:T(8,128)} %broadcast_in_dim.5), calls=%async_computation.4 | async-start | bytes 524288 | tf_op jit(solution)/shard_map/all_to_all | solution.py:232
  109.6 0.8 pad_maximum_fusion.1
  110.3 2.5 %collective-permute-start.8 = (f32[2,3,4,4,8,128]{5,4,3,2,1,0:T(8,128)}, f32[2,3,4,4,8,128]{5,4,3,2,1,0:T(8,128)S(1)}, u32[]{:S(2)}, u32[]{:S(2)}) collective-permute-start(f32[2,3,4,4,8,128]{5,4,3,2,1,0:T(8,128)} %pad_maximum_fusion.1), channel_id=1, source_target_pairs={{0,4},{4,0},{1,5},{5,1},{2,6},{6,2},{3,7},{7,3},{8,12},{12,8},{9,1... | collective-permute-start | bytes 1179656 | tf_op jit(solution)/shard_map/ppermute | solution.py:312
  112.9 3.3 %collective-permute-start.9 = (f32[2,3,4,4,8,128]{5,4,3,2,1,0:T(8,128)}, f32[2,3,4,4,8,128]{5,4,3,2,1,0:T(8,128)S(1)}, u32[]{:S(2)}, u32[]{:S(2)}) collective-permute-start(f32[2,3,4,4,8,128]{5,4,3,2,1,0:T(8,128)} %pad_maximum_fusion), channel_id=1, source_target_pairs={{0,4},{4,0},{1,5},{5,1},{2,6},{6,2},{3,7},{7,3},{8,12},{12,8},{9,1... | collective-permute-start | bytes 1179656 | tf_op jit(solution)/shard_map/ppermute | solution.py:326
  116.2 1.0 slice.51.weight_ref
  117.2 0.6 shard_map.117.gate_ref
  117.8 1.1 all-to-all-done.4.refs_6_
  118.8 5.6 %collective-permute-done.8.refs_4_ = f32[2,3,4,4,8,128]{5,4,3,2,1,0:T(8,128)S(1)} collective-permute-done((f32[2,3,4,4,8,128]{5,4,3,2,1,0:T(8,128)}, f32[2,3,4,4,8,128]{5,4,3,2,1,0:T(8,128)S(1)}, u32[]{:S(2)}, u32[]{:S(2)}) %collective-permute-start.8) | collective-permute-done | bytes 393248 | tf_op jit(solution)/shard_map/ppermute | solution.py:312
  124.4 6.6 %collective-permute-done.9.refs_5_ = f32[2,3,4,4,8,128]{5,4,3,2,1,0:T(8,128)S(1)} collective-permute-done((f32[2,3,4,4,8,128]{5,4,3,2,1,0:T(8,128)}, f32[2,3,4,4,8,128]{5,4,3,2,1,0:T(8,128)S(1)}, u32[]{:S(2)}, u32[]{:S(2)}) %collective-permute-start.9) | collective-permute-done | bytes 393248 | tf_op jit(solution)/shard_map/ppermute | solution.py:326
  131.0 4.6 %shard_map.118 = f32[32,4,8,128]{3,2,1,0:T(8,128)S(1)} custom-call(s32[3]{0:T(128)S(1)} %pad_add_fusion.own_ref.order_ref, f32[3,4,4,8,128]{4,3,2,1,0:T(8,128)S(1)} %get-tuple-element.34.refs_0_, f32[3,4,4,8,128]{4,3,2,1,0:T(8,128)S(1)} %get-tuple-element.35.refs_1_, f32[3,4,4,8,128]{4,3,2,1,0:T(8,128)S(1)} %get-tuple-element.36.refs_2_, ...), custom_call_target="tpu_custom_call" | custom-call | flops 4000000000 | bytes 1048576 | tf_op jit(solution)/shard_map/pallas_call | solution.py:221
  135.6 21.9 %all_to_all.35 = f32[32,4,8,128]{3,2,1,0:T(8,128)S(1)} all-to-all(f32[32,4,8,128]{3,2,1,0:T(8,128)S(1)} %shard_map.118), channel_id=1, replica_groups=mesh['xh'=2,'yh'=4,'yl'=2,'zh'=4,'zl'=2,'xl'=2,'core'=2] {'zh','zl','xl'..., dimensions={0} | all-to-all | bytes 1048576 | tf_op jit(solution)/shard_map/all_to_all | solution.py:232
  157.6 1.4 shard_map.119
  (32 shorter events, 0.2 us)
Async XLA Ops:
  0.6 29.6 %all-to-all-start = ((f32[4,16,8,256]{3,2,1,0:T(8,128)}), f32[4,16,8,256]{3,2,1,0:T(8,128)S(1)}, u32[]{:S(2)}, u32[]{:S(2)}) async-start(f32[4,16,8,256]{3,2,1,0:T(8,128)} %bitcast.49), calls=%async_computation | async-start | bytes 1048576 | tf_op jit(solution)/shard_map/all_to_all | solution.py:232
  10.9 1.1 copy-start
  12.0 0.8 copy-start.7
  12.9 0.7 copy-start.8
  13.5 12.8 %copy-start.10 = (f32[256,1024]{1,0:T(8,128)S(1)}, f32[256,1024]{1,0:T(8,128)}, u32[]{:S(2)}) copy-start(f32[256,1024]{1,0:T(8,128)} %param.18) | copy-start | bytes 3145732
  14.4 3.1 %collective-permute-start.2 = (f32[64,256]{1,0:T(8,128)S(1)}, f32[64,256]{1,0:T(8,128)S(1)}, u32[]{:S(2)}, u32[]{:S(2)}) collective-permute-start(f32[64,256]{1,0:T(8,128)S(1)} %get-tuple-element.30), channel_id=1, source_target_pairs={{0,1},{1,0},{2,3},{3,2},{4,5},{5,4},{6,7},{7,6},{8,9},{9,8},{10,11... | collective-permute-start | bytes 196616 | tf_op jit(solution)/shard_map/ppermute | solution.py:271
  17.5 9.0 %collective-permute-start.3 = (f32[2,64,256]{2,1,0:T(8,128)S(1)}, f32[2,64,256]{2,1,0:T(8,128)S(1)}, u32[]{:S(2)}, u32[]{:S(2)}) collective-permute-start(f32[2,64,256]{2,1,0:T(8,128)S(1)} %maximum_select_fusion.1), channel_id=1, source_target_pairs={{0,2},{2,0},{1,3},{3,1},{4,6},{6,4},{5,7},{7,5},{8,10},{10,8},{9,1... | collective-permute-start | bytes 393224 | tf_op jit(solution)/shard_map/ppermute | solution.py:276
  20.3 9.4 %collective-permute-start = (f32[64,128]{1,0:T(8,128)S(1)}, f32[64,128]{1,0:T(8,128)S(1)}, u32[]{:S(2)}, u32[]{:S(2)}) collective-permute-start(f32[64,128]{1,0:T(8,128)S(1)} %get-tuple-element.57), channel_id=1, source_target_pairs={{0,0},{2,32},{32,2},{34,34},{1,1},{3,33},{33,3},{35,35},{4,4},{6,3... | collective-permute-start | bytes 98312 | tf_op jit(solution)/shard_map/ppermute | solution.py:268
  24.4 5.8 %collective-permute-start.1 = (f32[64,128]{1,0:T(8,128)S(1)}, f32[64,128]{1,0:T(8,128)S(1)}, u32[]{:S(2)}, u32[]{:S(2)}) collective-permute-start(f32[64,128]{1,0:T(8,128)S(1)} %get-tuple-element.56), channel_id=1, source_target_pairs={{0,2},{2,34},{32,0},{34,32},{1,3},{3,35},{33,1},{35,33},{4,6},{6,3... | collective-permute-start | bytes 98312 | tf_op jit(solution)/shard_map/ppermute | solution.py:269
  26.4 11.9 %copy-start.9 = (f32[256]{0:T(256)S(1)}, f32[256]{0:T(256)}, u32[]{:S(2)}) copy-start(f32[256]{0:T(256)} %param.17) | copy-start | bytes 3076
  26.6 19.8 %collective-permute-start.4 = (f32[4,64,256]{2,1,0:T(8,128)S(1)}, f32[4,64,256]{2,1,0:T(8,128)S(1)}, u32[]{:S(2)}, u32[]{:S(2)}) collective-permute-start(f32[4,64,256]{2,1,0:T(8,128)S(1)} %maximum_select_fusion.own_ref), channel_id=1, source_target_pairs={{0,32},{32,0},{1,33},{33,1},{2,34},{34,2},{3,35},{35,3},{4,36},{36... | collective-permute-start | bytes 786440 | tf_op jit(solution)/shard_map/ppermute | solution.py:278
  31.1 23.5 %all-to-all-start.1 = ((f32[8,2,64,128]{3,2,1,0:T(8,128)}), f32[8,2,64,128]{3,2,1,0:T(8,128)S(1)}, u32[]{:S(2)}, u32[]{:S(2)}) async-start(f32[8,2,64,128]{3,2,1,0:T(8,128)} %broadcast_in_dim.4), calls=%async_computation.1 | async-start | bytes 1048576 | tf_op jit(solution)/shard_map/all_to_all | solution.py:232
  40.4 14.1 %copy-start.5 = (f32[1024,128]{1,0:T(8,128)S(1)}, f32[1024,128]{1,0:T(8,128)}, u32[]{:S(2)}) copy-start(f32[1024,128]{1,0:T(8,128)} %weight_ref.2) | copy-start | bytes 1572868
  41.4 18.6 %collective-permute-start.5 = (f32[2,2,3,4,4,8,128]{6,5,4,3,2,1,0:T(8,128)}, f32[2,2,3,4,4,8,128]{6,5,4,3,2,1,0:T(8,128)S(1)}, u32[]{:S(2)}, u32[]{:S(2)}) collective-permute-start(f32[2,2,3,4,4,8,128]{6,5,4,3,2,1,0:T(8,128)} %slice_bitcast_fusion), channel_id=1, source_target_pairs={{0,1},{1,0},{2,3},{3,2},{4,5},{5,4},{6,7},{7,6},{8,9},{9,8},{10,11... | collective-permute-start | bytes 2359304 | tf_op jit(solution)/shard_map/ppermute | solution.py:290
  44.1 28.8 %collective-permute-start.6 = (f32[2,3,4,4,8,128]{5,4,3,2,1,0:T(8,128)}, f32[2,3,4,4,8,128]{5,4,3,2,1,0:T(8,128)S(1)}, u32[]{:S(2)}, u32[]{:S(2)}) collective-permute-start(f32[2,3,4,4,8,128]{5,4,3,2,1,0:T(8,128)} %slice_bitcast_fusion.2), channel_id=1, source_target_pairs={{0,2},{2,0},{1,3},{3,1},{4,6},{6,4},{5,7},{7,5},{8,10},{10,8},{9,1... | collective-permute-start | bytes 1179656 | tf_op jit(solution)/shard_map/ppermute | solution.py:291
  60.0 27.8 %all-to-all-start.2 = ((f32[32,4,8,128]{3,2,1,0:T(8,128)}), f32[32,4,8,128]{3,2,1,0:T(8,128)S(1)}, u32[]{:S(2)}, u32[]{:S(2)}) async-start(f32[32,4,8,128]{3,2,1,0:T(8,128)} %bitcast.16), calls=%async_computation.2 | async-start | bytes 1048576 | tf_op jit(solution)/shard_map/all_to_all | solution.py:232
  70.0 17.8 %copy-start.2 = (f32[16,8,128]{2,1,0:T(8,128)S(1)}, f32[16,8,128]{2,1,0:T(8,128)}, u32[]{:S(2)}) copy-start(f32[16,8,128]{2,1,0:T(8,128)} %pair_ref.1) | copy-start | bytes 196612
  70.0 17.8 %copy-start.3 = (f32[128,8]{0,1:T(8,128)S(1)}, f32[128,8]{0,1:T(8,128)}, u32[]{:S(2)}) copy-start(f32[128,8]{0,1:T(8,128)} %param.16) | copy-start | bytes 12292
  70.0 17.8 %copy-start.4 = (f32[128]{0:T(128)S(1)}, f32[128]{0:T(128)}, u32[]{:S(2)}) copy-start(f32[128]{0:T(128)} %param.15) | copy-start | bytes 1540
  70.0 17.0 %collective-permute-start.7 = (f32[2,3,4,4,8,128]{5,4,3,2,1,0:T(8,128)S(1)}, f32[2,3,4,4,8,128]{5,4,3,2,1,0:T(8,128)S(1)}, u32[]{:S(2)}, u32[]{:S(2)}) collective-permute-start(f32[2,3,4,4,8,128]{5,4,3,2,1,0:T(8,128)S(1)} %slice_bitcast_fusion.1), channel_id=1, source_target_pairs={{0,2},{2,0},{1,3},{3,1},{4,6},{6,4},{5,7},{7,5},{8,10},{10,8},{9,1... | collective-permute-start | bytes 1179656 | tf_op jit(solution)/shard_map/ppermute | solution.py:311
  87.8 29.4 %copy-start.1 = (f32[64,8,256]{2,1,0:T(8,128)S(1)}, f32[64,8,256]{2,1,0:T(8,128)}, u32[]{:S(2)}) copy-start(f32[64,8,256]{2,1,0:T(8,128)} %param.10) | copy-start | bytes 1572868
  100.5 18.3 %all-to-all-start.4 = ((f32[16,16,256]{2,1,0:T(8,128)}), f32[16,16,256]{2,1,0:T(8,128)S(1)}, u32[]{:S(2)}, u32[]{:S(2)}) async-start(f32[16,16,256]{2,1,0:T(8,128)} %broadcast_in_dim.5), calls=%async_computation.4 | async-start | bytes 524288 | tf_op jit(solution)/shard_map/all_to_all | solution.py:232
  110.3 14.1 %collective-permute-start.8 = (f32[2,3,4,4,8,128]{5,4,3,2,1,0:T(8,128)}, f32[2,3,4,4,8,128]{5,4,3,2,1,0:T(8,128)S(1)}, u32[]{:S(2)}, u32[]{:S(2)}) collective-permute-start(f32[2,3,4,4,8,128]{5,4,3,2,1,0:T(8,128)} %pad_maximum_fusion.1), channel_id=1, source_target_pairs={{0,4},{4,0},{1,5},{5,1},{2,6},{6,2},{3,7},{7,3},{8,12},{12,8},{9,1... | collective-permute-start | bytes 1179656 | tf_op jit(solution)/shard_map/ppermute | solution.py:312
  112.9 18.2 %collective-permute-start.9 = (f32[2,3,4,4,8,128]{5,4,3,2,1,0:T(8,128)}, f32[2,3,4,4,8,128]{5,4,3,2,1,0:T(8,128)S(1)}, u32[]{:S(2)}, u32[]{:S(2)}) collective-permute-start(f32[2,3,4,4,8,128]{5,4,3,2,1,0:T(8,128)} %pad_maximum_fusion), channel_id=1, source_target_pairs={{0,4},{4,0},{1,5},{5,1},{2,6},{6,2},{3,7},{7,3},{8,12},{12,8},{9,1... | collective-permute-start | bytes 1179656 | tf_op jit(solution)/shard_map/ppermute | solution.py:326
  117.8 39.8 %copy-start.6 = (f32[256,256]{1,0:T(8,128)S(1)}, f32[256,256]{1,0:T(8,128)}, u32[]{:S(2)}) copy-start(f32[256,256]{1,0:T(8,128)} %weight_ref.3) | copy-start | bytes 786436

commit v3 on v2

--- a/solution.py
+++ b/solution.py
@@ -66,8 +66,8 @@
     return y
 
 
-def maps_kernel(rows_ref, gain_ref, weight_ref, left_ref, right_ref, maps_ref):
-    normed = center_scale(rows_ref[...]) * gain_ref[...]
+def maps_kernel(rows_ref, weight_ref, left_ref, right_ref, maps_ref):
+    normed = center_scale(rows_ref[...])
     maps_ref[:, :64] = dot6(normed, weight_ref[...], (((1,), (1,)), ((), ())))
     count = left_ref.shape[1]
     group = lane_group((count, 128))
@@ -258,8 +258,7 @@
         10**9,
         (shape_of(2, 64, 128), shape_of(64, 256)),
         rows,
-        outer_gain.reshape(1, 256),
-        w_outer_in.T,
+        w_outer_in.T * outer_gain[None],
         scratch=[pltpu.VMEM((512, 128), f32)],
     )
     moved_rows = exchanged(alignment.reshape(4, 16, 8, 256), "zh").reshape(512, 256)
@@ -274,8 +273,6 @@
     left = jnp.where(x == y, jnp.stack([left_a, left_b]), jnp.stack([left_b, left_a]))
     left_all = sent_to_all(left, ("zh", "zl")).reshape(8, 2, 64, 128)
     other = lax.ppermute(right, "xl", swap)
-    right = jnp.where(x == 0, jnp.concatenate([right, other]), jnp.concatenate([other, right]))
-    other = lax.ppermute(right, "yl", swap)
     qkv = call(
         project_kernel,
         4 * 10**9,
@@ -286,6 +283,9 @@
         w_project[:, :768],
         scalars=1,
     )
+    other, qkv = lax.optimization_barrier((other, qkv))
+    right = jnp.where(x == 0, jnp.concatenate([right, other]), jnp.concatenate([other, right]))
+    other = lax.ppermute(right, "yl", swap)
     order, qkv = lax.optimization_barrier((own, qkv))
     far_core = lax.ppermute(qkv[1], "core", swap)
     far_x = lax.ppermute(qkv[0, 1], "xl", swap)

time: 160 us -> 157 us (0.981)
  waiting for transfers between devices: 37.2 us -> 33.5 us
    all_to_all x4, waiting for transfers between devices: 9.27 us -> 6.6 us  [exchanged(): return lax.all_to_all(value, axes, 0, 0, tiled=True)]
  transfers between devices with their start and end apart: 14 -> 14, of which waited for: 7 -> 7; matrix products, arithmetic and copies ran while one was open for 3% -> 4% of each run, Pallas kernels for 6% -> 6%
where the time goes in v3:
time: 157 us; the launch traced here: 156 us
  starting transfers between devices  64.2 us (41%)
  waiting for transfers between devices  33.5 us (21%)
  blocking collectives  32.9 us (21%)
  Pallas kernels  15.8 us (10%)
  local copies, waits for them, and re-layouts  6.67 us (4%)
  other arithmetic  1.77 us (1%)
    all_to_all x4, starting transfers between devices, exchanged(): return lax.all_to_all(value, axes, 0, 0, tiled=True)  36.4 us
    all_to_all x2, blocking collectives, exchanged(): return lax.all_to_all(value, axes, 0, 0, tiled=True)  32.9 us
    pallas_call x7, Pallas kernels, call(): pl.pallas_call(kernel, in_specs=specs, out_shape=out_shape, scratch_shape...  15.8 us
    ppermute x1, waiting for transfers between devices, on_device(): last = lax.ppermute(far_core[1], 'xl', swap)  12.9 us
    ppermute x1, waiting for transfers between devices, on_device(): pieces = kept + [moved, lax.ppermute(sent, 'zl', swap)]  6.62 us
    all_to_all x4, waiting for transfers between devices, exchanged(): return lax.all_to_all(value, axes, 0, 0, tiled=True)  6.6 us
    ppermute x1, waiting for transfers between devices, on_device(): moved = lax.ppermute(jnp.stack([qkv[0, 0, 1], far_x[1]]), 'zl', swap)  5.59 us
    ppermute x1, starting transfers between devices, on_device(): other = lax.ppermute(right, 'xl', swap)  3.92 us
  transfers between devices with their start and end apart: 14, of which 7 were waited for; matrix products, arithmetic and copies ran while one was open for 4% of the time, Pallas kernels for 6%

profile of v3, /device:TPU:6, one launch (start us, length us, event | category | flops | bytes accessed | tf_op | source)
XLA Modules:
  0.0 155.8 jit_solution(17792426071613134795)
XLA Ops:
  0.6 10.3 %all-to-all-start = ((f32[4,16,8,256]{3,2,1,0:T(8,128)}), f32[4,16,8,256]{3,2,1,0:T(8,128)S(1)}, u32[]{:S(2)}, u32[]{:S(2)}) async-start(f32[4,16,8,256]{3,2,1,0:T(8,128)} %bitcast.49), calls=%async_computation | async-start | bytes 1048576 | tf_op jit(solution)/shard_map/all_to_all | solution.py:232
  10.9 0.8 multiply_bitcast_fusion.weight_ref
  11.8 1.0 copy-done
  12.8 0.8 shard_map.113
  13.7 3.8 %collective-permute-start.2 = (f32[64,128]{1,0:T(8,128)S(1)}, f32[64,128]{1,0:T(8,128)S(1)}, u32[]{:S(2)}, u32[]{:S(2)}) collective-permute-start(f32[64,128]{1,0:T(8,128)S(1)} %get-tuple-element.61), channel_id=1, source_target_pairs={{0,0},{2,32},{32,2},{34,34},{1,1},{3,33},{33,3},{35,35},{4,4},{6,3... | collective-permute-start | bytes 98312 | tf_op jit(solution)/shard_map/ppermute | solution.py:267
  17.4 1.9 %collective-permute-start.3 = (f32[64,128]{1,0:T(8,128)S(1)}, f32[64,128]{1,0:T(8,128)S(1)}, u32[]{:S(2)}, u32[]{:S(2)}) collective-permute-start(f32[64,128]{1,0:T(8,128)S(1)} %get-tuple-element.60), channel_id=1, source_target_pairs={{0,2},{2,34},{32,0},{34,32},{1,3},{3,35},{33,1},{35,33},{4,6},{6,3... | collective-permute-start | bytes 98312 | tf_op jit(solution)/shard_map/ppermute | solution.py:268
  19.4 1.9 %collective-permute-start = (f32[64,256]{1,0:T(8,128)S(1)}, f32[64,256]{1,0:T(8,128)S(1)}, u32[]{:S(2)}, u32[]{:S(2)}) collective-permute-start(f32[64,256]{1,0:T(8,128)S(1)} %get-tuple-element.27), channel_id=1, source_target_pairs={{0,1},{1,0},{2,3},{3,2},{4,5},{5,4},{6,7},{7,6},{8,9},{9,8},{10,11... | collective-permute-start | bytes 196616 | tf_op jit(solution)/shard_map/ppermute | solution.py:270
  21.3 0.0 copy-start.7
  21.3 0.1 slice.39.weight_ref
  21.4 0.1 pad_add_fusion.own_ref.order_ref
  21.5 1.0 collective-permute-done
  22.5 3.9 %collective-permute-start.1 = (f32[2,64,256]{2,1,0:T(8,128)S(1)}, f32[2,64,256]{2,1,0:T(8,128)S(1)}, u32[]{:S(2)}, u32[]{:S(2)}) collective-permute-start(f32[2,64,256]{2,1,0:T(8,128)S(1)} %maximum_select_fusion.1), channel_id=1, source_target_pairs={{0,2},{2,0},{1,3},{3,1},{4,6},{6,4},{5,7},{7,5},{8,10},{10,8},{9,1... | collective-permute-start | bytes 393224 | tf_op jit(solution)/shard_map/ppermute | solution.py:275
  26.5 0.8 broadcast_in_dim.4
  27.4 7.2 %all-to-all-start.1 = ((f32[8,2,64,128]{3,2,1,0:T(8,128)}), f32[8,2,64,128]{3,2,1,0:T(8,128)S(1)}, u32[]{:S(2)}, u32[]{:S(2)}) async-start(f32[8,2,64,128]{3,2,1,0:T(8,128)} %broadcast_in_dim.4), calls=%async_computation.1 | async-start | bytes 1048576 | tf_op jit(solution)/shard_map/all_to_all | solution.py:232
  34.6 2.1 %shard_map.114 = f32[2,2,2,3,4,4,8,128]{7,6,5,4,3,2,1,0:T(8,128)S(1)} custom-call(s32[3]{0:T(128)S(1)} %pad_add_fusion.own_ref.order_ref, f32[512,256]{1,0:T(8,128)S(1)} %bitcast.53, f32[1,256]{1,0:T(1,128)S(1)} %bitcast.59, f32[256,768]{1,0:T(8,128)S(1)} %slice.39.weight_ref), custom_call_target="tpu_custom_call" | custom-call | flops 4000000000 | bytes 1048576 | tf_op jit(solution)/shard_map/pallas_call | solution.py:221
  36.7 2.1 %collective-permute-start.4 = (f32[4,64,256]{2,1,0:T(8,128)S(1)}, f32[4,64,256]{2,1,0:T(8,128)S(1)}, u32[]{:S(2)}, u32[]{:S(2)}) collective-permute-start(f32[4,64,256]{2,1,0:T(8,128)S(1)} %maximum_select_fusion.own_ref), channel_id=1, source_target_pairs={{0,32},{32,0},{1,33},{33,1},{2,34},{34,2},{3,35},{35,3},{4,36},{36... | collective-permute-start | bytes 786440 | tf_op jit(solution)/shard_map/ppermute | solution.py:288
  38.8 0.1 slice_bitcast_fusion
  38.9 1.9 %collective-permute-start.5 = (f32[2,2,3,4,4,8,128]{6,5,4,3,2,1,0:T(8,128)S(1)}, f32[2,2,3,4,4,8,128]{6,5,4,3,2,1,0:T(8,128)S(1)}, u32[]{:S(2)}, u32[]{:S(2)}) collective-permute-start(f32[2,2,3,4,4,8,128]{6,5,4,3,2,1,0:T(8,128)S(1)} %slice_bitcast_fusion), channel_id=1, source_target_pairs={{0,1},{1,0},{2,3},{3,2},{4,5},{5,4},{6,7},{7,6},{8,9},{9,8},{10,11... | collective-permute-start | bytes 2359304 | tf_op jit(solution)/shard_map/ppermute | solution.py:290
  40.8 0.8 slice_bitcast_fusion.2
  41.6 3.5 %collective-permute-start.6 = (f32[2,3,4,4,8,128]{5,4,3,2,1,0:T(8,128)}, f32[2,3,4,4,8,128]{5,4,3,2,1,0:T(8,128)}, u32[]{:S(2)}, u32[]{:S(2)}) collective-permute-start(f32[2,3,4,4,8,128]{5,4,3,2,1,0:T(8,128)} %slice_bitcast_fusion.2), channel_id=1, source_target_pairs={{0,2},{2,0},{1,3},{3,1},{4,6},{6,4},{5,7},{7,5},{8,10},{10,8},{9,1... | collective-permute-start | bytes 1179656 | tf_op jit(solution)/shard_map/ppermute | solution.py:291
  45.1 0.7 slice_bitcast_fusion.5
  45.8 0.7 collective-permute-done.4.other_ref
  46.6 5.5 %all-to-all-done.1.left_ref = f32[8,2,64,128]{3,2,1,0:T(8,128)S(1)} async-done(((f32[8,2,64,128]{3,2,1,0:T(8,128)}), f32[8,2,64,128]{3,2,1,0:T(8,128)S(1)}, u32[]{:S(2)}, u32[]{:S(2)}) %all-to-all-start.1) | async-done | bytes 524320 | tf_op jit(solution)/shard_map/all_to_all | solution.py:232
  52.1 5.4 %shard_map.115 = f32[8,4,4,8,128]{4,3,2,1,0:T(8,128)} custom-call(s32[3]{0:T(128)S(1)} %pad_add_fusion.own_ref.order_ref, f32[8,2,64,128]{3,2,1,0:T(8,128)S(1)} %all-to-all-done.1.left_ref, f32[4,64,256]{2,1,0:T(8,128)S(1)} %maximum_select_fusion.own_ref, f32[4,64,256]{2,1,0:T(8,128)S(1)} %collective-permute-done.4.other_ref, f32[1024,128]{1,0:T(8,128)S(1)} %copy-done.5), custom_call_target="tpu_custom_call" | custom-call | flops 4000000000 | bytes 1048576 | tf_op jit(solution)/shard_map/pallas_call | solution.py:221
  57.5 9.0 %all-to-all-start.2 = ((f32[32,4,8,128]{3,2,1,0:T(8,128)}), f32[32,4,8,128]{3,2,1,0:T(8,128)S(1)}, u32[]{:S(2)}, u32[]{:S(2)}) async-start(f32[32,4,8,128]{3,2,1,0:T(8,128)} %bitcast.15), calls=%async_computation.2 | async-start | bytes 1048576 | tf_op jit(solution)/shard_map/all_to_all | solution.py:232
  66.6 0.0 copy-start.2
  66.6 0.0 copy-start.3
  66.6 2.9 %collective-permute-start.7 = (f32[2,3,4,4,8,128]{5,4,3,2,1,0:T(8,128)S(1)}, f32[2,3,4,4,8,128]{5,4,3,2,1,0:T(8,128)S(1)}, u32[]{:S(2)}, u32[]{:S(2)}) collective-permute-start(f32[2,3,4,4,8,128]{5,4,3,2,1,0:T(8,128)S(1)} %slice_bitcast_fusion.1), channel_id=1, source_target_pairs={{0,2},{2,0},{1,3},{3,1},{4,6},{6,4},{5,7},{7,5},{8,10},{10,8},{9,1... | collective-permute-start | bytes 1179656 | tf_op jit(solution)/shard_map/ppermute | solution.py:311
  69.6 1.0 fusion
  70.7 12.9 %collective-permute-done.7 = f32[2,3,4,4,8,128]{5,4,3,2,1,0:T(8,128)S(1)} collective-permute-done((f32[2,3,4,4,8,128]{5,4,3,2,1,0:T(8,128)S(1)}, f32[2,3,4,4,8,128]{5,4,3,2,1,0:T(8,128)S(1)}, u32[]{:S(2)}, u32[]{:S(2)}) %collective-permute-start.7) | collective-permute-done | bytes 393248 | tf_op jit(solution)/shard_map/ppermute | solution.py:311
  83.7 0.8 shard_map.116
  84.5 10.9 %all_to_all.34 = f32[32,1,128]{2,1,0:T(1,128)S(1)} all-to-all(f32[32,1,128]{2,1,0:T(1,128)S(1)} %bitcast.56), channel_id=1, replica_groups=mesh['xh'=2,'yh'=4,'yl'=2,'zh'=4,'zl'=2,'xl'=2,'core'=2] {'zh','zl','xl'..., dimensions={0} | all-to-all | bytes 32768 | tf_op jit(solution)/shard_map/all_to_all | solution.py:232
  95.5 0.1 copy.17
  95.5 0.1 copy.18
  95.7 0.1 copy.19
  95.7 0.7 broadcast_in_dim.5
  96.5 9.8 %all-to-all-start.4 = ((f32[16,16,256]{2,1,0:T(8,128)}), f32[16,16,256]{2,1,0:T(8,128)S(1)}, u32[]{:S(2)}, u32[]{:S(2)}) async-start(f32[16,16,256]{2,1,0:T(8,128)} %broadcast_in_dim.5), calls=%async_computation.4 | async-start | bytes 524288 | tf_op jit(solution)/shard_map/all_to_all | solution.py:232
  106.3 0.8 pad_maximum_fusion.1
  107.1 2.5 %collective-permute-start.8 = (f32[2,3,4,4,8,128]{5,4,3,2,1,0:T(8,128)}, f32[2,3,4,4,8,128]{5,4,3,2,1,0:T(8,128)S(1)}, u32[]{:S(2)}, u32[]{:S(2)}) collective-permute-start(f32[2,3,4,4,8,128]{5,4,3,2,1,0:T(8,128)} %pad_maximum_fusion.1), channel_id=1, source_target_pairs={{0,4},{4,0},{1,5},{5,1},{2,6},{6,2},{3,7},{7,3},{8,12},{12,8},{9,1... | collective-permute-start | bytes 1179656 | tf_op jit(solution)/shard_map/ppermute | solution.py:312
  109.6 3.3 %collective-permute-start.9 = (f32[2,3,4,4,8,128]{5,4,3,2,1,0:T(8,128)S(1)}, f32[2,3,4,4,8,128]{5,4,3,2,1,0:T(8,128)S(1)}, u32[]{:S(2)}, u32[]{:S(2)}) collective-permute-start(f32[2,3,4,4,8,128]{5,4,3,2,1,0:T(8,128)S(1)} %pad_maximum_fusion), channel_id=1, source_target_pairs={{0,4},{4,0},{1,5},{5,1},{2,6},{6,2},{3,7},{7,3},{8,12},{12,8},{9,1... | collective-permute-start | bytes 1179656 | tf_op jit(solution)/shard_map/ppermute | solution.py:326
  112.9 1.0 slice.51.weight_ref
  113.9 0.6 shard_map.117.gate_ref
  114.5 1.0 all-to-all-done.4.refs_6_
  115.6 5.6 %collective-permute-done.8.refs_4_ = f32[2,3,4,4,8,128]{5,4,3,2,1,0:T(8,128)S(1)} collective-permute-done((f32[2,3,4,4,8,128]{5,4,3,2,1,0:T(8,128)}, f32[2,3,4,4,8,128]{5,4,3,2,1,0:T(8,128)S(1)}, u32[]{:S(2)}, u32[]{:S(2)}) %collective-permute-start.8) | collective-permute-done | bytes 393248 | tf_op jit(solution)/shard_map/ppermute | solution.py:312
  121.2 6.6 %collective-permute-done.9.refs_5_ = f32[2,3,4,4,8,128]{5,4,3,2,1,0:T(8,128)S(1)} collective-permute-done((f32[2,3,4,4,8,128]{5,4,3,2,1,0:T(8,128)S(1)}, f32[2,3,4,4,8,128]{5,4,3,2,1,0:T(8,128)S(1)}, u32[]{:S(2)}, u32[]{:S(2)}) %collective-permute-start.9) | collective-permute-done | bytes 393248 | tf_op jit(solution)/shard_map/ppermute | solution.py:326
  127.8 4.6 %shard_map.118 = f32[32,4,8,128]{3,2,1,0:T(8,128)S(1)} custom-call(s32[3]{0:T(128)S(1)} %pad_add_fusion.own_ref.order_ref, f32[3,4,4,8,128]{4,3,2,1,0:T(8,128)S(1)} %get-tuple-element.38.refs_0_, f32[3,4,4,8,128]{4,3,2,1,0:T(8,128)S(1)} %get-tuple-element.39.refs_1_, f32[3,4,4,8,128]{4,3,2,1,0:T(8,128)S(1)} %get-tuple-element.40.refs_2_, ...), custom_call_target="tpu_custom_call" | custom-call | flops 4000000000 | bytes 1048576 | tf_op jit(solution)/shard_map/pallas_call | solution.py:221
  132.4 21.9 %all_to_all.35 = f32[32,4,8,128]{3,2,1,0:T(8,128)S(1)} all-to-all(f32[32,4,8,128]{3,2,1,0:T(8,128)S(1)} %shard_map.118), channel_id=1, replica_groups=mesh['xh'=2,'yh'=4,'yl'=2,'zh'=4,'zl'=2,'xl'=2,'core'=2] {'zh','zl','xl'..., dimensions={0} | all-to-all | bytes 1048576 | tf_op jit(solution)/shard_map/all_to_all | solution.py:232
  154.4 1.4 shard_map.119
  (31 shorter events, 0.2 us)
Async XLA Ops:
  0.6 25.9 %all-to-all-start = ((f32[4,16,8,256]{3,2,1,0:T(8,128)}), f32[4,16,8,256]{3,2,1,0:T(8,128)S(1)}, u32[]{:S(2)}, u32[]{:S(2)}) async-start(f32[4,16,8,256]{3,2,1,0:T(8,128)} %bitcast.49), calls=%async_computation | async-start | bytes 1048576 | tf_op jit(solution)/shard_map/all_to_all | solution.py:232
  11.8 1.0 copy-start
  12.8 8.5 %copy-start.8 = (f32[256,1024]{1,0:T(8,128)S(1)}, f32[256,1024]{1,0:T(8,128)}, u32[]{:S(2)}) copy-start(f32[256,1024]{1,0:T(8,128)} %param.18) | copy-start | bytes 3145732
  13.7 12.8 %collective-permute-start.2 = (f32[64,128]{1,0:T(8,128)S(1)}, f32[64,128]{1,0:T(8,128)S(1)}, u32[]{:S(2)}, u32[]{:S(2)}) collective-permute-start(f32[64,128]{1,0:T(8,128)S(1)} %get-tuple-element.61), channel_id=1, source_target_pairs={{0,0},{2,32},{32,2},{34,34},{1,1},{3,33},{33,3},{35,35},{4,4},{6,3... | collective-permute-start | bytes 98312 | tf_op jit(solution)/shard_map/ppermute | solution.py:267
  17.4 9.0 %collective-permute-start.3 = (f32[64,128]{1,0:T(8,128)S(1)}, f32[64,128]{1,0:T(8,128)S(1)}, u32[]{:S(2)}, u32[]{:S(2)}) collective-permute-start(f32[64,128]{1,0:T(8,128)S(1)} %get-tuple-element.60), channel_id=1, source_target_pairs={{0,2},{2,34},{32,0},{34,32},{1,3},{3,35},{33,1},{35,33},{4,6},{6,3... | collective-permute-start | bytes 98312 | tf_op jit(solution)/shard_map/ppermute | solution.py:268
  19.4 3.1 %collective-permute-start = (f32[64,256]{1,0:T(8,128)S(1)}, f32[64,256]{1,0:T(8,128)S(1)}, u32[]{:S(2)}, u32[]{:S(2)}) collective-permute-start(f32[64,256]{1,0:T(8,128)S(1)} %get-tuple-element.27), channel_id=1, source_target_pairs={{0,1},{1,0},{2,3},{3,2},{4,5},{5,4},{6,7},{7,6},{8,9},{9,8},{10,11... | collective-permute-start | bytes 196616 | tf_op jit(solution)/shard_map/ppermute | solution.py:270
  21.3 13.3 %copy-start.7 = (f32[256]{0:T(256)S(1)}, f32[256]{0:T(256)}, u32[]{:S(2)}) copy-start(f32[256]{0:T(256)} %param.17) | copy-start | bytes 3076
  22.5 14.1 %collective-permute-start.1 = (f32[2,64,256]{2,1,0:T(8,128)S(1)}, f32[2,64,256]{2,1,0:T(8,128)S(1)}, u32[]{:S(2)}, u32[]{:S(2)}) collective-permute-start(f32[2,64,256]{2,1,0:T(8,128)S(1)} %maximum_select_fusion.1), channel_id=1, source_target_pairs={{0,2},{2,0},{1,3},{3,1},{4,6},{6,4},{5,7},{7,5},{8,10},{10,8},{9,1... | collective-permute-start | bytes 393224 | tf_op jit(solution)/shard_map/ppermute | solution.py:275
  27.4 24.8 %all-to-all-start.1 = ((f32[8,2,64,128]{3,2,1,0:T(8,128)}), f32[8,2,64,128]{3,2,1,0:T(8,128)S(1)}, u32[]{:S(2)}, u32[]{:S(2)}) async-start(f32[8,2,64,128]{3,2,1,0:T(8,128)} %broadcast_in_dim.4), calls=%async_computation.1 | async-start | bytes 1048576 | tf_op jit(solution)/shard_map/all_to_all | solution.py:232
  36.7 15.4 %copy-start.5 = (f32[1024,128]{1,0:T(8,128)S(1)}, f32[1024,128]{1,0:T(8,128)}, u32[]{:S(2)}) copy-start(f32[1024,128]{1,0:T(8,128)} %weight_ref.2) | copy-start | bytes 1572868
  36.7 9.8 %collective-permute-start.4 = (f32[4,64,256]{2,1,0:T(8,128)S(1)}, f32[4,64,256]{2,1,0:T(8,128)S(1)}, u32[]{:S(2)}, u32[]{:S(2)}) collective-permute-start(f32[4,64,256]{2,1,0:T(8,128)S(1)} %maximum_select_fusion.own_ref), channel_id=1, source_target_pairs={{0,32},{32,0},{1,33},{33,1},{2,34},{34,2},{3,35},{35,3},{4,36},{36... | collective-permute-start | bytes 786440 | tf_op jit(solution)/shard_map/ppermute | solution.py:288
  38.9 18.7 %collective-permute-start.5 = (f32[2,2,3,4,4,8,128]{6,5,4,3,2,1,0:T(8,128)S(1)}, f32[2,2,3,4,4,8,128]{6,5,4,3,2,1,0:T(8,128)S(1)}, u32[]{:S(2)}, u32[]{:S(2)}) collective-permute-start(f32[2,2,3,4,4,8,128]{6,5,4,3,2,1,0:T(8,128)S(1)} %slice_bitcast_fusion), channel_id=1, source_target_pairs={{0,1},{1,0},{2,3},{3,2},{4,5},{5,4},{6,7},{7,6},{8,9},{9,8},{10,11... | collective-permute-start | bytes 2359304 | tf_op jit(solution)/shard_map/ppermute | solution.py:290
  41.6 28.0 %collective-permute-start.6 = (f32[2,3,4,4,8,128]{5,4,3,2,1,0:T(8,128)}, f32[2,3,4,4,8,128]{5,4,3,2,1,0:T(8,128)}, u32[]{:S(2)}, u32[]{:S(2)}) collective-permute-start(f32[2,3,4,4,8,128]{5,4,3,2,1,0:T(8,128)} %slice_bitcast_fusion.2), channel_id=1, source_target_pairs={{0,2},{2,0},{1,3},{3,1},{4,6},{6,4},{5,7},{7,5},{8,10},{10,8},{9,1... | collective-permute-start | bytes 1179656 | tf_op jit(solution)/shard_map/ppermute | solution.py:291
  57.5 26.1 %all-to-all-start.2 = ((f32[32,4,8,128]{3,2,1,0:T(8,128)}), f32[32,4,8,128]{3,2,1,0:T(8,128)S(1)}, u32[]{:S(2)}, u32[]{:S(2)}) async-start(f32[32,4,8,128]{3,2,1,0:T(8,128)} %bitcast.15), calls=%async_computation.2 | async-start | bytes 1048576 | tf_op jit(solution)/shard_map/all_to_all | solution.py:232
  66.6 17.0 %copy-start.2 = (f32[16,8,128]{2,1,0:T(8,128)S(1)}, f32[16,8,128]{2,1,0:T(8,128)}, u32[]{:S(2)}) copy-start(f32[16,8,128]{2,1,0:T(8,128)} %pair_ref.1) | copy-start | bytes 196612
  66.6 17.0 %copy-start.3 = (f32[128,8]{0,1:T(8,128)S(1)}, f32[128,8]{0,1:T(8,128)}, u32[]{:S(2)}) copy-start(f32[128,8]{0,1:T(8,128)} %param.16) | copy-start | bytes 12292
  66.6 17.0 %copy-start.4 = (f32[128]{0:T(128)S(1)}, f32[128]{0:T(128)}, u32[]{:S(2)}) copy-start(f32[128]{0:T(128)} %param.15) | copy-start | bytes 1540
  66.6 16.9 %collective-permute-start.7 = (f32[2,3,4,4,8,128]{5,4,3,2,1,0:T(8,128)S(1)}, f32[2,3,4,4,8,128]{5,4,3,2,1,0:T(8,128)S(1)}, u32[]{:S(2)}, u32[]{:S(2)}) collective-permute-start(f32[2,3,4,4,8,128]{5,4,3,2,1,0:T(8,128)S(1)} %slice_bitcast_fusion.1), channel_id=1, source_target_pairs={{0,2},{2,0},{1,3},{3,1},{4,6},{6,4},{5,7},{7,5},{8,10},{10,8},{9,1... | collective-permute-start | bytes 1179656 | tf_op jit(solution)/shard_map/ppermute | solution.py:311
  70.7 35.7 %copy-start.9 = (f32[1,3,4,4,8,128]{5,4,3,2,1,0:T(8,128)S(1)}, f32[1,3,4,4,8,128]{5,4,3,2,1,0:T(8,128)}, u32[]{:S(2)}) copy-start(f32[1,3,4,4,8,128]{5,4,3,2,1,0:T(8,128)} %get-tuple-element.52) | copy-start | bytes 589828
  83.7 30.2 %copy-start.1 = (f32[64,8,256]{2,1,0:T(8,128)S(1)}, f32[64,8,256]{2,1,0:T(8,128)}, u32[]{:S(2)}) copy-start(f32[64,8,256]{2,1,0:T(8,128)} %param.10) | copy-start | bytes 1572868
  96.5 19.1 %all-to-all-start.4 = ((f32[16,16,256]{2,1,0:T(8,128)}), f32[16,16,256]{2,1,0:T(8,128)S(1)}, u32[]{:S(2)}, u32[]{:S(2)}) async-start(f32[16,16,256]{2,1,0:T(8,128)} %broadcast_in_dim.5), calls=%async_computation.4 | async-start | bytes 524288 | tf_op jit(solution)/shard_map/all_to_all | solution.py:232
  107.1 14.1 %collective-permute-start.8 = (f32[2,3,4,4,8,128]{5,4,3,2,1,0:T(8,128)}, f32[2,3,4,4,8,128]{5,4,3,2,1,0:T(8,128)S(1)}, u32[]{:S(2)}, u32[]{:S(2)}) collective-permute-start(f32[2,3,4,4,8,128]{5,4,3,2,1,0:T(8,128)} %pad_maximum_fusion.1), channel_id=1, source_target_pairs={{0,4},{4,0},{1,5},{5,1},{2,6},{6,2},{3,7},{7,3},{8,12},{12,8},{9,1... | collective-permute-start | bytes 1179656 | tf_op jit(solution)/shard_map/ppermute | solution.py:312
  109.6 18.2 %collective-permute-start.9 = (f32[2,3,4,4,8,128]{5,4,3,2,1,0:T(8,128)S(1)}, f32[2,3,4,4,8,128]{5,4,3,2,1,0:T(8,128)S(1)}, u32[]{:S(2)}, u32[]{:S(2)}) collective-permute-start(f32[2,3,4,4,8,128]{5,4,3,2,1,0:T(8,128)S(1)} %pad_maximum_fusion), channel_id=1, source_target_pairs={{0,4},{4,0},{1,5},{5,1},{2,6},{6,2},{3,7},{7,3},{8,12},{12,8},{9,1... | collective-permute-start | bytes 1179656 | tf_op jit(solution)/shard_map/ppermute | solution.py:326
  114.5 39.9 %copy-start.6 = (f32[256,256]{1,0:T(8,128)S(1)}, f32[256,256]{1,0:T(8,128)}, u32[]{:S(2)}) copy-start(f32[256,256]{1,0:T(8,128)} %weight_ref.3) | copy-start | bytes 786436

commit v4 on v3

--- a/solution.py
+++ b/solution.py
@@ -103,8 +103,15 @@
     gate_ref[...] = jax.nn.sigmoid(dot3(normed, weight_ref[...]))
 
 
+def weight_kernel(weight_ref, both_ref):
+    for y in range(32):
+        high, low = halves(weight_ref[pl.ds(y, 32, stride=32), :])
+        both_ref[y * 32 : y * 32 + 32, :128] = high
+        both_ref[y * 32 : y * 32 + 32, 128:] = low
+
+
 def outer_kernel(
-    order_ref, left_ref, own_ref, other_ref, weight_ref, out_ref, turned_ref, rows_ref, parts_ref, both_ref
+    order_ref, left_ref, own_ref, other_ref, both_ref, out_ref, turned_ref, rows_ref, parts_ref
 ):
     for r in range(4):
         both = jnp.concatenate([own_ref[r], other_ref[r]], axis=0)
@@ -115,10 +122,6 @@
     high, low = halves(rows_ref[...])
     parts_ref[:, :128] = high
     parts_ref[:, 128:] = low
-    for y in range(32):
-        high, low = halves(weight_ref[pl.ds(y, 32, stride=32), :])
-        both_ref[y * 32 : y * 32 + 32, :128] = high
-        both_ref[y * 32 : y * 32 + 32, 128:] = low
     dot = functools.partial(jnp.dot, preferred_element_type=f32)
 
     for z in range(4):
@@ -286,6 +289,8 @@
     other, qkv = lax.optimization_barrier((other, qkv))
     right = jnp.where(x == 0, jnp.concatenate([right, other]), jnp.concatenate([other, right]))
     other = lax.ppermute(right, "yl", swap)
+    late_weight, qkv = lax.optimization_barrier((w_outer_out, qkv))
+    both = call(weight_kernel, 10**6, jax.ShapeDtypeStruct((1024, 256), bf16), late_weight)
     order, qkv = lax.optimization_barrier((own, qkv))
     far_core = lax.ppermute(qkv[1], "core", swap)
     far_x = lax.ppermute(qkv[0, 1], "xl", swap)
@@ -297,11 +302,10 @@
         left_all,
         right,
         other,
-        w_outer_out,
+        both,
         scratch=[
             pltpu.VMEM((4, 256, 128), f32),
             pltpu.VMEM((1024, 128), f32),
-            pltpu.VMEM((1024, 256), bf16),
             pltpu.VMEM((1024, 256), bf16),
         ],
         scalars=1,

time: 157 us -> 157 us (level)
    pallas_call x7 -> x8, Pallas kernels: 15.8 us -> 16 us  [call(): pl.pallas_call(kernel, in_specs=specs, out_shape=out_shape, scratch_shape...]
where the time goes in v4:
time: 157 us; the launch traced here: 156 us
  starting transfers between devices  64.1 us (41%)
  waiting for transfers between devices  34 us (22%)
  blocking collectives  33 us (21%)
  Pallas kernels  16 us (10%)
  local copies, waits for them, and re-layouts  5.87 us (4%)
  other arithmetic  2.51 us (2%)
    all_to_all x4, starting transfers between devices, exchanged(): return lax.all_to_all(value, axes, 0, 0, tiled=True)  36.3 us
    all_to_all x2, blocking collectives, exchanged(): return lax.all_to_all(value, axes, 0, 0, tiled=True)  33 us
    pallas_call x8, Pallas kernels, call(): pl.pallas_call(kernel, in_specs=specs, out_shape=out_shape, scratch_shape...  16 us
    ppermute x1, waiting for transfers between devices, on_device(): last = lax.ppermute(far_core[1], 'xl', swap)  13.9 us
    ppermute x1, waiting for transfers between devices, on_device(): pieces = kept + [moved, lax.ppermute(sent, 'zl', swap)]  6.62 us
    all_to_all x4, waiting for transfers between devices, exchanged(): return lax.all_to_all(value, axes, 0, 0, tiled=True)  6.61 us
    ppermute x1, waiting for transfers between devices, on_device(): moved = lax.ppermute(jnp.stack([qkv[0, 0, 1], far_x[1]]), 'zl', swap)  5.58 us
    ppermute x1, starting transfers between devices, on_device(): other = lax.ppermute(right, 'xl', swap)  3.92 us
  transfers between devices with their start and end apart: 14, of which 7 were waited for; matrix products, arithmetic and copies ran while one was open for 4% of the time, Pallas kernels for 6%

profile of v4, /device:TPU:6, one launch (start us, length us, event | category | flops | bytes accessed | tf_op | source)
XLA Modules:
  0.0 156.3 jit_solution(5940753142729230281)
XLA Ops:
  0.6 10.3 %all-to-all-start = ((f32[4,16,8,256]{3,2,1,0:T(8,128)}), f32[4,16,8,256]{3,2,1,0:T(8,128)S(1)}, u32[]{:S(2)}, u32[]{:S(2)}) async-start(f32[4,16,8,256]{3,2,1,0:T(8,128)} %bitcast.49), calls=%async_computation | async-start | bytes 1048576 | tf_op jit(solution)/shard_map/all_to_all | solution.py:235
  10.9 0.8 multiply_bitcast_fusion.weight_ref
  11.8 1.0 copy-done.1
  12.8 0.8 shard_map.113
  13.7 3.8 %collective-permute-start.2 = (f32[64,128]{1,0:T(8,128)S(1)}, f32[64,128]{1,0:T(8,128)S(1)}, u32[]{:S(2)}, u32[]{:S(2)}) collective-permute-start(f32[64,128]{1,0:T(8,128)S(1)} %get-tuple-element.65), channel_id=1, source_target_pairs={{0,0},{2,32},{32,2},{34,34},{1,1},{3,33},{33,3},{35,35},{4,4},{6,3... | collective-permute-start | bytes 98312 | tf_op jit(solution)/shard_map/ppermute | solution.py:270
  17.4 1.9 %collective-permute-start.3 = (f32[64,128]{1,0:T(8,128)S(1)}, f32[64,128]{1,0:T(8,128)S(1)}, u32[]{:S(2)}, u32[]{:S(2)}) collective-permute-start(f32[64,128]{1,0:T(8,128)S(1)} %get-tuple-element.64), channel_id=1, source_target_pairs={{0,2},{2,34},{32,0},{34,32},{1,3},{3,35},{33,1},{35,33},{4,6},{6,3... | collective-permute-start | bytes 98312 | tf_op jit(solution)/shard_map/ppermute | solution.py:271
  19.4 1.9 %collective-permute-start = (f32[64,256]{1,0:T(8,128)S(1)}, f32[64,256]{1,0:T(8,128)S(1)}, u32[]{:S(2)}, u32[]{:S(2)}) collective-permute-start(f32[64,256]{1,0:T(8,128)S(1)} %get-tuple-element.29), channel_id=1, source_target_pairs={{0,1},{1,0},{2,3},{3,2},{4,5},{5,4},{6,7},{7,6},{8,9},{9,8},{10,11... | collective-permute-start | bytes 196616 | tf_op jit(solution)/shard_map/ppermute | solution.py:273
  21.3 0.0 copy-start.7
  21.3 0.1 slice.39.weight_ref
  21.4 0.1 pad_add_fusion.own_ref.order_ref
  21.5 1.0 collective-permute-done
  22.5 3.9 %collective-permute-start.1 = (f32[2,64,256]{2,1,0:T(8,128)S(1)}, f32[2,64,256]{2,1,0:T(8,128)S(1)}, u32[]{:S(2)}, u32[]{:S(2)}) collective-permute-start(f32[2,64,256]{2,1,0:T(8,128)S(1)} %maximum_select_fusion.1), channel_id=1, source_target_pairs={{0,2},{2,0},{1,3},{3,1},{4,6},{6,4},{5,7},{7,5},{8,10},{10,8},{9,1... | collective-permute-start | bytes 393224 | tf_op jit(solution)/shard_map/ppermute | solution.py:278
  26.5 0.8 broadcast_in_dim.4
  27.4 7.2 %all-to-all-start.1 = ((f32[8,2,64,128]{3,2,1,0:T(8,128)}), f32[8,2,64,128]{3,2,1,0:T(8,128)S(1)}, u32[]{:S(2)}, u32[]{:S(2)}) async-start(f32[8,2,64,128]{3,2,1,0:T(8,128)} %broadcast_in_dim.4), calls=%async_computation.1 | async-start | bytes 1048576 | tf_op jit(solution)/shard_map/all_to_all | solution.py:235
  34.6 2.1 %shard_map.114 = f32[2,2,2,3,4,4,8,128]{7,6,5,4,3,2,1,0:T(8,128)S(1)} custom-call(s32[3]{0:T(128)S(1)} %pad_add_fusion.own_ref.order_ref, f32[512,256]{1,0:T(8,128)S(1)} %bitcast.53, f32[1,256]{1,0:T(1,128)S(1)} %bitcast.59, f32[256,768]{1,0:T(8,128)S(1)} %slice.39.weight_ref), custom_call_target="tpu_custom_call" | custom-call | flops 4000000000 | bytes 1048576 | tf_op jit(solution)/shard_map/pallas_call | solution.py:224
  36.7 2.1 %collective-permute-start.4 = (f32[4,64,256]{2,1,0:T(8,128)S(1)}, f32[4,64,256]{2,1,0:T(8,128)S(1)}, u32[]{:S(2)}, u32[]{:S(2)}) collective-permute-start(f32[4,64,256]{2,1,0:T(8,128)S(1)} %maximum_select_fusion.own_ref), channel_id=1, source_target_pairs={{0,32},{32,0},{1,33},{33,1},{2,34},{34,2},{3,35},{35,3},{4,36},{36... | collective-permute-start | bytes 786440 | tf_op jit(solution)/shard_map/ppermute | solution.py:291
  38.8 1.0 slice_bitcast_fusion
  39.8 1.9 %collective-permute-start.5 = (f32[2,2,3,4,4,8,128]{6,5,4,3,2,1,0:T(8,128)}, f32[2,2,3,4,4,8,128]{6,5,4,3,2,1,0:T(8,128)S(1)}, u32[]{:S(2)}, u32[]{:S(2)}) collective-permute-start(f32[2,2,3,4,4,8,128]{6,5,4,3,2,1,0:T(8,128)} %slice_bitcast_fusion), channel_id=1, source_target_pairs={{0,1},{1,0},{2,3},{3,2},{4,5},{5,4},{6,7},{7,6},{8,9},{9,8},{10,11... | collective-permute-start | bytes 2359304 | tf_op jit(solution)/shard_map/ppermute | solution.py:295
  41.7 0.8 slice_bitcast_fusion.2
  42.5 3.5 %collective-permute-start.6 = (f32[2,3,4,4,8,128]{5,4,3,2,1,0:T(8,128)}, f32[2,3,4,4,8,128]{5,4,3,2,1,0:T(8,128)S(1)}, u32[]{:S(2)}, u32[]{:S(2)}) collective-permute-start(f32[2,3,4,4,8,128]{5,4,3,2,1,0:T(8,128)} %slice_bitcast_fusion.2), channel_id=1, source_target_pairs={{0,2},{2,0},{1,3},{3,1},{4,6},{6,4},{5,7},{7,5},{8,10},{10,8},{9,1... | collective-permute-start | bytes 1179656 | tf_op jit(solution)/shard_map/ppermute | solution.py:296
  46.0 0.3 shard_map.115.both_ref
  46.4 0.2 collective-permute-done.4.other_ref
  46.6 5.5 %all-to-all-done.1.left_ref = f32[8,2,64,128]{3,2,1,0:T(8,128)S(1)} async-done(((f32[8,2,64,128]{3,2,1,0:T(8,128)}), f32[8,2,64,128]{3,2,1,0:T(8,128)S(1)}, u32[]{:S(2)}, u32[]{:S(2)}) %all-to-all-start.1) | async-done | bytes 524320 | tf_op jit(solution)/shard_map/all_to_all | solution.py:235
  52.1 5.2 %shard_map.116 = f32[8,4,4,8,128]{4,3,2,1,0:T(8,128)} custom-call(s32[3]{0:T(128)S(1)} %pad_add_fusion.own_ref.order_ref, f32[8,2,64,128]{3,2,1,0:T(8,128)S(1)} %all-to-all-done.1.left_ref, f32[4,64,256]{2,1,0:T(8,128)S(1)} %maximum_select_fusion.own_ref, f32[4,64,256]{2,1,0:T(8,128)S(1)} %collective-permute-done.4.other_ref, ...), custom_call_target="tpu_custom_call" | custom-call | flops 4000000000 | bytes 1048576 | tf_op jit(solution)/shard_map/pallas_call | solution.py:224
  57.4 9.0 %all-to-all-start.2 = ((f32[32,4,8,128]{3,2,1,0:T(8,128)}), f32[32,4,8,128]{3,2,1,0:T(8,128)S(1)}, u32[]{:S(2)}, u32[]{:S(2)}) async-start(f32[32,4,8,128]{3,2,1,0:T(8,128)} %bitcast.15), calls=%async_computation.2 | async-start | bytes 1048576 | tf_op jit(solution)/shard_map/all_to_all | solution.py:235
  66.4 0.0 copy-start.3
  66.5 0.0 copy-start.5
  66.5 2.9 %collective-permute-start.7 = (f32[2,3,4,4,8,128]{5,4,3,2,1,0:T(8,128)S(1)}, f32[2,3,4,4,8,128]{5,4,3,2,1,0:T(8,128)S(1)}, u32[]{:S(2)}, u32[]{:S(2)}) collective-permute-start(f32[2,3,4,4,8,128]{5,4,3,2,1,0:T(8,128)S(1)} %slice_bitcast_fusion.1), channel_id=1, source_target_pairs={{0,2},{2,0},{1,3},{3,1},{4,6},{6,4},{5,7},{7,5},{8,10},{10,8},{9,1... | collective-permute-start | bytes 1179656 | tf_op jit(solution)/shard_map/ppermute | solution.py:315
  69.5 13.9 %collective-permute-done.7 = f32[2,3,4,4,8,128]{5,4,3,2,1,0:T(8,128)S(1)} collective-permute-done((f32[2,3,4,4,8,128]{5,4,3,2,1,0:T(8,128)S(1)}, f32[2,3,4,4,8,128]{5,4,3,2,1,0:T(8,128)S(1)}, u32[]{:S(2)}, u32[]{:S(2)}) %collective-permute-start.7) | collective-permute-done | bytes 393248 | tf_op jit(solution)/shard_map/ppermute | solution.py:315
  83.4 0.8 pad_maximum_fusion
  84.2 0.8 shard_map.117
  85.1 11.0 %all_to_all.34 = f32[32,1,128]{2,1,0:T(1,128)S(1)} all-to-all(f32[32,1,128]{2,1,0:T(1,128)S(1)} %bitcast.56), channel_id=1, replica_groups=mesh['xh'=2,'yh'=4,'yl'=2,'zh'=4,'zl'=2,'xl'=2,'core'=2] {'zh','zl','xl'..., dimensions={0} | all-to-all | bytes 32768 | tf_op jit(solution)/shard_map/all_to_all | solution.py:235
  96.1 0.1 copy.17
  96.2 0.1 copy.18
  96.3 0.1 copy.19
  96.4 0.7 broadcast_in_dim.5
  97.1 9.8 %all-to-all-start.4 = ((f32[16,16,256]{2,1,0:T(8,128)}), f32[16,16,256]{2,1,0:T(8,128)S(1)}, u32[]{:S(2)}, u32[]{:S(2)}) async-start(f32[16,16,256]{2,1,0:T(8,128)} %broadcast_in_dim.5), calls=%async_computation.4 | async-start | bytes 524288 | tf_op jit(solution)/shard_map/all_to_all | solution.py:235
  106.9 0.8 pad_maximum_fusion.1
  107.6 2.5 %collective-permute-start.8 = (f32[2,3,4,4,8,128]{5,4,3,2,1,0:T(8,128)}, f32[2,3,4,4,8,128]{5,4,3,2,1,0:T(8,128)S(1)}, u32[]{:S(2)}, u32[]{:S(2)}) collective-permute-start(f32[2,3,4,4,8,128]{5,4,3,2,1,0:T(8,128)} %pad_maximum_fusion.1), channel_id=1, source_target_pairs={{0,4},{4,0},{1,5},{5,1},{2,6},{6,2},{3,7},{7,3},{8,12},{12,8},{9,1... | collective-permute-start | bytes 1179656 | tf_op jit(solution)/shard_map/ppermute | solution.py:316
  110.1 3.3 %collective-permute-start.9 = (f32[2,3,4,4,8,128]{5,4,3,2,1,0:T(8,128)}, f32[2,3,4,4,8,128]{5,4,3,2,1,0:T(8,128)S(1)}, u32[]{:S(2)}, u32[]{:S(2)}) collective-permute-start(f32[2,3,4,4,8,128]{5,4,3,2,1,0:T(8,128)} %pad_maximum_fusion), channel_id=1, source_target_pairs={{0,4},{4,0},{1,5},{5,1},{2,6},{6,2},{3,7},{7,3},{8,12},{12,8},{9,1... | collective-permute-start | bytes 1179656 | tf_op jit(solution)/shard_map/ppermute | solution.py:330
  113.5 1.0 slice.51.weight_ref
  114.5 0.6 shard_map.118.gate_ref
  115.1 1.1 all-to-all-done.4.refs_6_
  116.1 5.6 %collective-permute-done.8.refs_4_ = f32[2,3,4,4,8,128]{5,4,3,2,1,0:T(8,128)S(1)} collective-permute-done((f32[2,3,4,4,8,128]{5,4,3,2,1,0:T(8,128)}, f32[2,3,4,4,8,128]{5,4,3,2,1,0:T(8,128)S(1)}, u32[]{:S(2)}, u32[]{:S(2)}) %collective-permute-start.8) | collective-permute-done | bytes 393248 | tf_op jit(solution)/shard_map/ppermute | solution.py:316
  121.7 6.6 %collective-permute-done.9.refs_5_ = f32[2,3,4,4,8,128]{5,4,3,2,1,0:T(8,128)S(1)} collective-permute-done((f32[2,3,4,4,8,128]{5,4,3,2,1,0:T(8,128)}, f32[2,3,4,4,8,128]{5,4,3,2,1,0:T(8,128)S(1)}, u32[]{:S(2)}, u32[]{:S(2)}) %collective-permute-start.9) | collective-permute-done | bytes 393248 | tf_op jit(solution)/shard_map/ppermute | solution.py:330
  128.3 4.6 %shard_map.119 = f32[32,4,8,128]{3,2,1,0:T(8,128)S(1)} custom-call(s32[3]{0:T(128)S(1)} %pad_add_fusion.own_ref.order_ref, f32[3,4,4,8,128]{4,3,2,1,0:T(8,128)S(1)} %get-tuple-element.42.refs_0_, f32[3,4,4,8,128]{4,3,2,1,0:T(8,128)S(1)} %get-tuple-element.43.refs_1_, f32[3,4,4,8,128]{4,3,2,1,0:T(8,128)S(1)} %get-tuple-element.44.refs_2_, ...), custom_call_target="tpu_custom_call" | custom-call | flops 4000000000 | bytes 1048576 | tf_op jit(solution)/shard_map/pallas_call | solution.py:224
  133.0 21.9 %all_to_all.35 = f32[32,4,8,128]{3,2,1,0:T(8,128)S(1)} all-to-all(f32[32,4,8,128]{3,2,1,0:T(8,128)S(1)} %shard_map.119), channel_id=1, replica_groups=mesh['xh'=2,'yh'=4,'yl'=2,'zh'=4,'zl'=2,'xl'=2,'core'=2] {'zh','zl','xl'..., dimensions={0} | all-to-all | bytes 1048576 | tf_op jit(solution)/shard_map/all_to_all | solution.py:235
  154.9 1.4 shard_map.120
  (30 shorter events, 0.2 us)
Async XLA Ops:
  0.6 25.9 %all-to-all-start = ((f32[4,16,8,256]{3,2,1,0:T(8,128)}), f32[4,16,8,256]{3,2,1,0:T(8,128)S(1)}, u32[]{:S(2)}, u32[]{:S(2)}) async-start(f32[4,16,8,256]{3,2,1,0:T(8,128)} %bitcast.49), calls=%async_computation | async-start | bytes 1048576 | tf_op jit(solution)/shard_map/all_to_all | solution.py:235
  11.8 1.0 copy-start.1
  12.8 8.5 %copy-start.8 = (f32[256,1024]{1,0:T(8,128)S(1)}, f32[256,1024]{1,0:T(8,128)}, u32[]{:S(2)}) copy-start(f32[256,1024]{1,0:T(8,128)} %param.18) | copy-start | bytes 3145732
  13.7 12.8 %collective-permute-start.2 = (f32[64,128]{1,0:T(8,128)S(1)}, f32[64,128]{1,0:T(8,128)S(1)}, u32[]{:S(2)}, u32[]{:S(2)}) collective-permute-start(f32[64,128]{1,0:T(8,128)S(1)} %get-tuple-element.65), channel_id=1, source_target_pairs={{0,0},{2,32},{32,2},{34,34},{1,1},{3,33},{33,3},{35,35},{4,4},{6,3... | collective-permute-start | bytes 98312 | tf_op jit(solution)/shard_map/ppermute | solution.py:270
  17.4 9.0 %collective-permute-start.3 = (f32[64,128]{1,0:T(8,128)S(1)}, f32[64,128]{1,0:T(8,128)S(1)}, u32[]{:S(2)}, u32[]{:S(2)}) collective-permute-start(f32[64,128]{1,0:T(8,128)S(1)} %get-tuple-element.64), channel_id=1, source_target_pairs={{0,2},{2,34},{32,0},{34,32},{1,3},{3,35},{33,1},{35,33},{4,6},{6,3... | collective-permute-start | bytes 98312 | tf_op jit(solution)/shard_map/ppermute | solution.py:271
  19.4 3.1 %collective-permute-start = (f32[64,256]{1,0:T(8,128)S(1)}, f32[64,256]{1,0:T(8,128)S(1)}, u32[]{:S(2)}, u32[]{:S(2)}) collective-permute-start(f32[64,256]{1,0:T(8,128)S(1)} %get-tuple-element.29), channel_id=1, source_target_pairs={{0,1},{1,0},{2,3},{3,2},{4,5},{5,4},{6,7},{7,6},{8,9},{9,8},{10,11... | collective-permute-start | bytes 196616 | tf_op jit(solution)/shard_map/ppermute | solution.py:273
  21.3 13.3 %copy-start.7 = (f32[256]{0:T(256)S(1)}, f32[256]{0:T(256)}, u32[]{:S(2)}) copy-start(f32[256]{0:T(256)} %param.17) | copy-start | bytes 3076
  22.5 14.2 %collective-permute-start.1 = (f32[2,64,256]{2,1,0:T(8,128)S(1)}, f32[2,64,256]{2,1,0:T(8,128)S(1)}, u32[]{:S(2)}, u32[]{:S(2)}) collective-permute-start(f32[2,64,256]{2,1,0:T(8,128)S(1)} %maximum_select_fusion.1), channel_id=1, source_target_pairs={{0,2},{2,0},{1,3},{3,1},{4,6},{6,4},{5,7},{7,5},{8,10},{10,8},{9,1... | collective-permute-start | bytes 393224 | tf_op jit(solution)/shard_map/ppermute | solution.py:278
  27.4 24.8 %all-to-all-start.1 = ((f32[8,2,64,128]{3,2,1,0:T(8,128)}), f32[8,2,64,128]{3,2,1,0:T(8,128)S(1)}, u32[]{:S(2)}, u32[]{:S(2)}) async-start(f32[8,2,64,128]{3,2,1,0:T(8,128)} %broadcast_in_dim.4), calls=%async_computation.1 | async-start | bytes 1048576 | tf_op jit(solution)/shard_map/all_to_all | solution.py:235
  36.7 9.3 %copy-start = (f32[1024,128]{1,0:T(8,128)S(1)}, f32[1024,128]{1,0:T(8,128)}, u32[]{:S(2)}) copy-start(f32[1024,128]{1,0:T(8,128)} %weight_ref.1) | copy-start | bytes 1572868
  36.7 9.8 %collective-permute-start.4 = (f32[4,64,256]{2,1,0:T(8,128)S(1)}, f32[4,64,256]{2,1,0:T(8,128)S(1)}, u32[]{:S(2)}, u32[]{:S(2)}) collective-permute-start(f32[4,64,256]{2,1,0:T(8,128)S(1)} %maximum_select_fusion.own_ref), channel_id=1, source_target_pairs={{0,32},{32,0},{1,33},{33,1},{2,34},{34,2},{3,35},{35,3},{4,36},{36... | collective-permute-start | bytes 786440 | tf_op jit(solution)/shard_map/ppermute | solution.py:291
  39.8 17.6 %collective-permute-start.5 = (f32[2,2,3,4,4,8,128]{6,5,4,3,2,1,0:T(8,128)}, f32[2,2,3,4,4,8,128]{6,5,4,3,2,1,0:T(8,128)S(1)}, u32[]{:S(2)}, u32[]{:S(2)}) collective-permute-start(f32[2,2,3,4,4,8,128]{6,5,4,3,2,1,0:T(8,128)} %slice_bitcast_fusion), channel_id=1, source_target_pairs={{0,1},{1,0},{2,3},{3,2},{4,5},{5,4},{6,7},{7,6},{8,9},{9,8},{10,11... | collective-permute-start | bytes 2359304 | tf_op jit(solution)/shard_map/ppermute | solution.py:295
  42.5 26.9 %collective-permute-start.6 = (f32[2,3,4,4,8,128]{5,4,3,2,1,0:T(8,128)}, f32[2,3,4,4,8,128]{5,4,3,2,1,0:T(8,128)S(1)}, u32[]{:S(2)}, u32[]{:S(2)}) collective-permute-start(f32[2,3,4,4,8,128]{5,4,3,2,1,0:T(8,128)} %slice_bitcast_fusion.2), channel_id=1, source_target_pairs={{0,2},{2,0},{1,3},{3,1},{4,6},{6,4},{5,7},{7,5},{8,10},{10,8},{9,1... | collective-permute-start | bytes 1179656 | tf_op jit(solution)/shard_map/ppermute | solution.py:296
  57.4 26.8 %all-to-all-start.2 = ((f32[32,4,8,128]{3,2,1,0:T(8,128)}), f32[32,4,8,128]{3,2,1,0:T(8,128)S(1)}, u32[]{:S(2)}, u32[]{:S(2)}) async-start(f32[32,4,8,128]{3,2,1,0:T(8,128)} %bitcast.15), calls=%async_computation.2 | async-start | bytes 1048576 | tf_op jit(solution)/shard_map/all_to_all | solution.py:235
  66.4 17.8 %copy-start.3 = (f32[16,8,128]{2,1,0:T(8,128)S(1)}, f32[16,8,128]{2,1,0:T(8,128)}, u32[]{:S(2)}) copy-start(f32[16,8,128]{2,1,0:T(8,128)} %pair_ref.1) | copy-start | bytes 196612
  66.5 17.7 %copy-start.4 = (f32[128,8]{0,1:T(8,128)S(1)}, f32[128,8]{0,1:T(8,128)}, u32[]{:S(2)}) copy-start(f32[128,8]{0,1:T(8,128)} %param.16) | copy-start | bytes 12292
  66.5 17.7 %copy-start.5 = (f32[128]{0:T(128)S(1)}, f32[128]{0:T(128)}, u32[]{:S(2)}) copy-start(f32[128]{0:T(128)} %param.15) | copy-start | bytes 1540
  66.5 16.9 %collective-permute-start.7 = (f32[2,3,4,4,8,128]{5,4,3,2,1,0:T(8,128)S(1)}, f32[2,3,4,4,8,128]{5,4,3,2,1,0:T(8,128)S(1)}, u32[]{:S(2)}, u32[]{:S(2)}) collective-permute-start(f32[2,3,4,4,8,128]{5,4,3,2,1,0:T(8,128)S(1)} %slice_bitcast_fusion.1), channel_id=1, source_target_pairs={{0,2},{2,0},{1,3},{3,1},{4,6},{6,4},{5,7},{7,5},{8,10},{10,8},{9,1... | collective-permute-start | bytes 1179656 | tf_op jit(solution)/shard_map/ppermute | solution.py:315
  84.2 30.2 %copy-start.2 = (f32[64,8,256]{2,1,0:T(8,128)S(1)}, f32[64,8,256]{2,1,0:T(8,128)}, u32[]{:S(2)}) copy-start(f32[64,8,256]{2,1,0:T(8,128)} %param.10) | copy-start | bytes 1572868
  97.1 19.0 %all-to-all-start.4 = ((f32[16,16,256]{2,1,0:T(8,128)}), f32[16,16,256]{2,1,0:T(8,128)S(1)}, u32[]{:S(2)}, u32[]{:S(2)}) async-start(f32[16,16,256]{2,1,0:T(8,128)} %broadcast_in_dim.5), calls=%async_computation.4 | async-start | bytes 524288 | tf_op jit(solution)/shard_map/all_to_all | solution.py:235
  107.6 14.1 %collective-permute-start.8 = (f32[2,3,4,4,8,128]{5,4,3,2,1,0:T(8,128)}, f32[2,3,4,4,8,128]{5,4,3,2,1,0:T(8,128)S(1)}, u32[]{:S(2)}, u32[]{:S(2)}) collective-permute-start(f32[2,3,4,4,8,128]{5,4,3,2,1,0:T(8,128)} %pad_maximum_fusion.1), channel_id=1, source_target_pairs={{0,4},{4,0},{1,5},{5,1},{2,6},{6,2},{3,7},{7,3},{8,12},{12,8},{9,1... | collective-permute-start | bytes 1179656 | tf_op jit(solution)/shard_map/ppermute | solution.py:316
  110.1 18.2 %collective-permute-start.9 = (f32[2,3,4,4,8,128]{5,4,3,2,1,0:T(8,128)}, f32[2,3,4,4,8,128]{5,4,3,2,1,0:T(8,128)S(1)}, u32[]{:S(2)}, u32[]{:S(2)}) collective-permute-start(f32[2,3,4,4,8,128]{5,4,3,2,1,0:T(8,128)} %pad_maximum_fusion), channel_id=1, source_target_pairs={{0,4},{4,0},{1,5},{5,1},{2,6},{6,2},{3,7},{7,3},{8,12},{12,8},{9,1... | collective-permute-start | bytes 1179656 | tf_op jit(solution)/shard_map/ppermute | solution.py:330
  115.1 39.9 %copy-start.6 = (f32[256,256]{1,0:T(8,128)S(1)}, f32[256,256]{1,0:T(8,128)}, u32[]{:S(2)}) copy-start(f32[256,256]{1,0:T(8,128)} %weight_ref.2) | copy-start | bytes 786436
